TPU v7x, 16 devices: a 4x2x1 block of a 4x4x8 slice. The times are simulated.
16 devices in a mesh: req: 2 (over y, z), cp: 8 (over x, core).
Axes of the slice: x: 4, y: 2, z: 1, core: 2. Of those that a mesh axis runs over, the one named last changes fastest.
The devices are a block of a 4x4x8 slice.
Arguments:
- hidden: bfloat16 [1024, 1536], P(('req', 'cp')), parts along dimension 0
- prefix_k: bfloat16 [4, 16384, 256], P(None, 'req', 'cp'), parts along dimension 1
- prefix_v: bfloat16 [4, 16384, 256], P(None, 'req', 'cp'), parts along dimension 1
- gain_attn: bfloat16 [4, 1536], replicated
- gain_mlp: bfloat16 [4, 1536], replicated
- w_query: bfloat16 [4, 1536, 12, 128], replicated
- w_key: bfloat16 [4, 1536, 2, 128], replicated
- w_value: bfloat16 [4, 1536, 2, 128], replicated
- w_out: bfloat16 [4, 12, 128, 1536], replicated
- w_gate: bfloat16 [4, 1536, 8960], replicated
- w_up: bfloat16 [4, 1536, 8960], replicated
- w_down: bfloat16 [4, 8960, 1536], replicated
Outputs:
- output 1: bfloat16 [1024, 1536], P(('req', 'cp')), parts along dimension 0
- output 2: bfloat16 [4, 17408, 256], P(None, 'req', 'cp'), parts along dimension 1
- output 3: bfloat16 [4, 17408, 256], P(None, 'req', 'cp'), parts along dimension 1
There are 2 independent parts. A program takes and returns all parts, laid end to end along the dimension named above; an argument that names none is the same for every part.
All inputs are finite; a program needn't handle non-finite values.
Results may differ from a plain program's by a relative error of at most 0.02.
Values are sent between devices in bfloat16 or wider.
A program may use at most 768 MiB of HBM per device.

v0:
```python
import jax
import jax.numpy as jnp
from jax import lax
from jax.sharding import PartitionSpec as P

NORM_EPS = 1e-5
ROPE_THETA = 500000.0


def rms_norm(hidden, gain):
    hidden_f32 = hidden.astype(jnp.float32)
    inv_rms = lax.rsqrt(jnp.mean(hidden_f32 * hidden_f32, axis=-1, keepdims=True) + NORM_EPS)
    return (hidden_f32 * inv_rms * gain.astype(jnp.float32)).astype(jnp.bfloat16)


def rope_tables(positions, head_dim):
    inv_freq = ROPE_THETA ** (-jnp.arange(0, head_dim, 2, dtype=jnp.float32) / head_dim)
    angles = positions.astype(jnp.float32)[:, None] * inv_freq[None, :]
    return jnp.cos(angles), jnp.sin(angles)


def rope_rotate(projected, cos_tab, sin_tab):
    half_dim = projected.shape[-1] // 2
    lower_half = projected[..., :half_dim]
    upper_half = projected[..., half_dim:]
    cos_part = cos_tab[:, None, :]
    sin_part = sin_tab[:, None, :]
    return jnp.concatenate([lower_half * cos_part - upper_half * sin_part, upper_half * cos_part + lower_half * sin_part], axis=-1)


def piece_positions(dev_ids, cp_size, half_piece, offset):
    piece_ids = jnp.stack([dev_ids, 2 * cp_size - 1 - dev_ids], axis=-1)
    return (offset + piece_ids[..., None] * half_piece + jnp.arange(half_piece)).reshape(-1)


def to_natural(row_data, cp_size):
    lead_dim, seq_len, num_cols = row_data.shape
    blocks = row_data.reshape(lead_dim, cp_size, 2, seq_len // (2 * cp_size), num_cols)
    return jnp.concatenate([blocks[:, :, 0], jnp.flip(blocks[:, :, 1], axis=1)], axis=1).reshape(lead_dim, seq_len, num_cols)


def local_attention(queries, keys_pre, values_pre, keys_new, values_new, allowed, head_dim):
    score_scale = head_dim ** -0.5
    scores_pre = jnp.einsum('tkgd,skd->kgts', queries, keys_pre, preferred_element_type=jnp.float32) * score_scale
    scores_new = jnp.einsum('tkgd,skd->kgts', queries, keys_new, preferred_element_type=jnp.float32) * score_scale
    scores_new = jnp.where(allowed, scores_new, -jnp.inf)
    row_max = jnp.maximum(scores_pre.max(axis=-1), scores_new.max(axis=-1))[..., None]
    exp_pre = jnp.exp(scores_pre - row_max)
    exp_new = jnp.exp(scores_new - row_max)
    denominator = (exp_pre.sum(axis=-1) + exp_new.sum(axis=-1))[..., None]
    probs_pre = (exp_pre / denominator).astype(jnp.bfloat16)
    probs_new = (exp_new / denominator).astype(jnp.bfloat16)
    attn_out = jnp.einsum('kgts,skd->tkgd', probs_pre, values_pre, preferred_element_type=jnp.float32) + jnp.einsum('kgts,skd->tkgd', probs_new, values_new, preferred_element_type=jnp.float32)
    return attn_out.astype(jnp.bfloat16)


def solution(mesh):
    cp_size = mesh.shape['cp']

    def device_fn(hidden, prefix_k, prefix_v, gain_attn, gain_mlp, w_query, w_key, w_value, w_out, w_gate, w_up, w_down):
        num_layers, d_model, kv_heads, head_dim = w_key.shape
        num_heads = w_query.shape[2]
        groups = num_heads // kv_heads
        tok_dev = hidden.shape[0]
        half_piece = tok_dev // 2
        prefix_len = prefix_k.shape[1]
        kv_dim = kv_heads * head_dim
        my_index = lax.axis_index('cp')
        query_pos = piece_positions(my_index, cp_size, half_piece, prefix_len)
        key_pos = piece_positions(jnp.arange(cp_size), cp_size, half_piece, prefix_len)
        allowed = key_pos[None, :] <= query_pos[:, None]
        cos_tab, sin_tab = rope_tables(query_pos, head_dim)
        keys_kept = []
        values_kept = []
        for layer_idx in range(num_layers):
            normed = rms_norm(hidden, gain_attn[layer_idx])
            queries = jnp.einsum('td,dhe->the', normed, w_query[layer_idx], preferred_element_type=jnp.float32)
            queries = rope_rotate(queries, cos_tab, sin_tab).astype(jnp.bfloat16).reshape(tok_dev, kv_heads, groups, head_dim)
            keys_loc = jnp.einsum('td,dke->tke', normed, w_key[layer_idx], preferred_element_type=jnp.float32)
            keys_loc = rope_rotate(keys_loc, cos_tab, sin_tab).astype(jnp.bfloat16)
            values_loc = jnp.einsum('td,dke->tke', normed, w_value[layer_idx], preferred_element_type=jnp.float32).astype(jnp.bfloat16)
            keys_new = lax.all_gather(keys_loc, 'cp', axis=0, tiled=True)
            values_new = lax.all_gather(values_loc, 'cp', axis=0, tiled=True)
            keys_pre = lax.all_gather(prefix_k[layer_idx], 'cp', axis=1, tiled=True).reshape(prefix_len, kv_heads, head_dim)
            values_pre = lax.all_gather(prefix_v[layer_idx], 'cp', axis=1, tiled=True).reshape(prefix_len, kv_heads, head_dim)
            attn_out = local_attention(queries, keys_pre, values_pre, keys_new, values_new, allowed, head_dim)
            attn_out = attn_out.reshape(tok_dev, num_heads, head_dim)
            hidden = (hidden.astype(jnp.float32) + jnp.einsum('the,hed->td', attn_out, w_out[layer_idx], preferred_element_type=jnp.float32)).astype(jnp.bfloat16)
            normed_mlp = rms_norm(hidden, gain_mlp[layer_idx])
            gate_proj = jnp.dot(normed_mlp, w_gate[layer_idx], preferred_element_type=jnp.float32)
            up_proj = jnp.dot(normed_mlp, w_up[layer_idx], preferred_element_type=jnp.float32)
            gated_act = (jax.nn.silu(gate_proj) * up_proj).astype(jnp.bfloat16)
            hidden = (hidden.astype(jnp.float32) + jnp.dot(gated_act, w_down[layer_idx], preferred_element_type=jnp.float32)).astype(jnp.bfloat16)
            keys_kept.append(keys_loc.reshape(tok_dev, kv_dim))
            values_kept.append(values_loc.reshape(tok_dev, kv_dim))
        keys_sent = lax.all_to_all(jnp.stack(keys_kept), 'cp', 2, 1, tiled=True)
        values_sent = lax.all_to_all(jnp.stack(values_kept), 'cp', 2, 1, tiled=True)
        cache_k = jnp.concatenate([prefix_k, to_natural(keys_sent, cp_size)], axis=1)
        cache_v = jnp.concatenate([prefix_v, to_natural(values_sent, cp_size)], axis=1)
        return hidden, cache_k, cache_v

    in_specs = (P(('req', 'cp'), None), P(None, 'req', 'cp'), P(None, 'req', 'cp')) + (P(),) * 9
    out_specs = (P(('req', 'cp'), None), P(None, 'req', 'cp'), P(None, 'req', 'cp'))
    return jax.shard_map(device_fn, mesh=mesh, in_specs=in_specs, out_specs=out_specs, check_vma=False)
```

profile of v0, /device:TPU:113, one launch (start us, length us, event | category | flops | bytes accessed | tf_op | source)
XLA Modules:
  0.0 560.0 jit_solution(10965474654486823403)
XLA Ops:
  20.5 21.7 %all_gather.51 = bf16[512,2,128]{2,0,1:T(8,128)(2,1)S(1)} all-gather(bf16[64,2,128]{2,0,1:T(8,128)(2,1)S(1)} %convolution_convert_fusion.3), channel_id=1, replica_groups=mesh['req'=2,'cp'=8] {'cp'}, dimensions={0}, use_global_device_ids=true | all-gather | bytes 294912 | tf_op jit(solution)/shard_map/all_gather | solution.py:83
  47.6 23.0 %all_gather.49 = bf16[512,2,128]{2,0,1:T(8,128)(2,1)S(1)} all-gather(bf16[64,2,128]{2,0,1:T(8,128)(2,1)S(1)} %maximum_convert_fusion), channel_id=1, replica_groups=mesh['req'=2,'cp'=8] {'cp'}, dimensions={0}, use_global_device_ids=true | all-gather | bytes 294912 | tf_op jit(solution)/shard_map/all_gather | solution.py:82
  77.0 12.7 %bitcast_reduce_fusion.3 = (f32[2,6,64]{2,1,0:T(8,128)S(1)}, f32[2,64,6,8192]{3,1,2,0:T(8,128)}) fusion(bf16[8192,2,128,1]{0,2,3,1:T(8,128)(2,1)} %bitcast.463, bf16[64,2,6,64]{3,0,2,1:T(8,128)(2,1)S(1)} %bitcast.469, bf16[64,2,6,64]{3,0,2,1:T(8,128)(2,1)S(1)} %bitcast.467), kind=kOutput, calls=%fused_computation.46 | convolution fusion | flops 1623588096 | bytes 29559808 | tf_op jit(solution)/shard_map/tkgd,skd->kgts/dot_general | solution.py:44
  101.1 11.8 %fusion.188 = f32[64,2,6,128]{3,0,2,1:T(8,128)S(1)} fusion(bf16[8192,2,128,1]{0,2,3,1:T(8,128)(2,1)} %bitcast.495, f32[2,64,6,8192]{3,1,2,0:T(8,128)} %get-tuple-element.50, f32[2,6,64]{2,1,0:T(8,128)S(1)} %add.238, f32[2,6,64]{2,1,0:T(8,128)S(1)} %max.28), kind=kOutput, calls=%fused_computation.148 | convolution fusion | flops 1635778560 | bytes 29759488 | tf_op jit(solution)/shard_map/kgts,skd->tkgd/dot_general | solution.py:53
  117.3 12.4 %fusion.22 = f32[64,8960]{1,0:T(8,128)} fusion(bf16[4,1536,8960]{2,1,0:T(8,128)(2,1)} %param.21, f32[64,1536]{1,0:T(8,128)S(1)} %get-tuple-element.54, f32[1536]{0:T(1024)S(1)} %get-tuple-element.5, f32[64]{0:T(128)S(1)} %add_rsqrt_fusion.6), kind=kOutput, calls=%fused_computation.22 | convolution fusion | flops 1761902592 | bytes 30218496 | tf_op jit(solution)/shard_map/dot_general | solution.py:90
  129.7 21.1 %multiply_reduce_fusion.5 = (f32[64]{0:T(128)S(1)}, f32[64,1536]{1,0:T(8,128)S(1)}) fusion(f32[64,1536]{1,0:T(8,128)S(1)} %get-tuple-element.54, bf16[4,8960,1536]{2,1,0:T(8,128)(2,1)} %param.23, bf16[4,1536,8960]{2,1,0:T(8,128)(2,1)} %param.22, f32[64,8960]{1,0:T(8,128)} %fusion.22, f32[1536]{0:T(1024)S(1)} %get-tuple-element.5, f32[64]{0:T(128)S(1)} %add_rsqrt_fusion.6), kind=kOutput, calls=%fused_computation.193 | convolution fusion | flops 3527442432 | bytes 58532608 | tf_op jit(solution)/shard_map/dot_general | solution.py:93
  155.3 21.3 %all_gather.53 = bf16[512,2,128]{2,0,1:T(8,128)(2,1)S(1)} all-gather(bf16[64,2,128]{2,0,1:T(8,128)(2,1)S(1)} %maximum_convert_fusion.1), channel_id=1, replica_groups=mesh['req'=2,'cp'=8] {'cp'}, dimensions={0}, use_global_device_ids=true | all-gather | bytes 294912 | tf_op jit(solution)/shard_map/all_gather | solution.py:82
  177.4 12.5 %bitcast_reduce_fusion.2 = (f32[2,6,64]{2,1,0:T(8,128)S(1)}, f32[2,64,6,8192]{3,1,2,0:T(8,128)}) fusion(bf16[8192,2,128,1]{0,2,3,1:T(8,128)(2,1)} %bitcast.462, bf16[64,2,6,64]{3,0,2,1:T(8,128)(2,1)S(1)} %bitcast.477, bf16[64,2,6,64]{3,0,2,1:T(8,128)(2,1)S(1)} %bitcast.475), kind=kOutput, calls=%fused_computation.43 | convolution fusion | flops 1623588096 | bytes 29559808 | tf_op jit(solution)/shard_map/tkgd,skd->kgts/dot_general | solution.py:44
  201.6 23.6 %all_gather.55 = bf16[512,2,128]{2,0,1:T(8,128)(2,1)S(1)} all-gather(bf16[64,2,128]{2,0,1:T(8,128)(2,1)S(1)} %convolution_convert_fusion.2), channel_id=1, replica_groups=mesh['req'=2,'cp'=8] {'cp'}, dimensions={0}, use_global_device_ids=true | all-gather | bytes 294912 | tf_op jit(solution)/shard_map/all_gather | solution.py:83
  225.2 11.8 %fusion.187 = f32[64,2,6,128]{3,0,2,1:T(8,128)S(1)} fusion(bf16[8192,2,128,1]{0,2,3,1:T(8,128)(2,1)} %bitcast.494, f32[2,64,6,8192]{3,1,2,0:T(8,128)} %get-tuple-element.58, f32[2,6,64]{2,1,0:T(8,128)S(1)} %add.247, f32[2,6,64]{2,1,0:T(8,128)S(1)} %max.29), kind=kOutput, calls=%fused_computation.147 | convolution fusion | flops 1635778560 | bytes 29759488 | tf_op jit(solution)/shard_map/kgts,skd->tkgd/dot_general | solution.py:53
  241.0 12.4 %fusion.16 = f32[64,8960]{1,0:T(8,128)} fusion(bf16[4,1536,8960]{2,1,0:T(8,128)(2,1)} %param.21, f32[64,1536]{1,0:T(8,128)S(1)} %get-tuple-element.62, f32[1536]{0:T(1024)S(1)} %copy-done.24, f32[64]{0:T(128)S(1)} %add_rsqrt_fusion.4), kind=kOutput, calls=%fused_computation.16 | convolution fusion | flops 1761902592 | bytes 30218496 | tf_op jit(solution)/shard_map/dot_general | solution.py:90
  253.3 21.2 %multiply_reduce_fusion.3 = (f32[64]{0:T(128)S(1)}, f32[64,1536]{1,0:T(8,128)S(1)}) fusion(f32[64,1536]{1,0:T(8,128)S(1)} %get-tuple-element.62, bf16[4,8960,1536]{2,1,0:T(8,128)(2,1)} %param.23, bf16[4,1536,8960]{2,1,0:T(8,128)(2,1)} %param.22, f32[64,8960]{1,0:T(8,128)} %fusion.16, f32[1536]{0:T(1024)S(1)} %copy-done.24, f32[64]{0:T(128)S(1)} %add_rsqrt_fusion.4), kind=kOutput, calls=%fused_computation.187 | convolution fusion | flops 3527442432 | bytes 58532608 | tf_op jit(solution)/shard_map/dot_general | solution.py:93
  278.4 21.2 %all_gather.57 = bf16[512,2,128]{2,0,1:T(8,128)(2,1)S(1)} all-gather(bf16[64,2,128]{2,0,1:T(8,128)(2,1)S(1)} %maximum_convert_fusion.2), channel_id=1, replica_groups=mesh['req'=2,'cp'=8] {'cp'}, dimensions={0}, use_global_device_ids=true | all-gather | bytes 294912 | tf_op jit(solution)/shard_map/all_gather | solution.py:82
  300.4 12.5 %bitcast_reduce_fusion.1 = (f32[2,6,64]{2,1,0:T(8,128)S(1)}, f32[2,64,6,8192]{3,1,2,0:T(8,128)}) fusion(bf16[8192,2,128,1]{0,2,3,1:T(8,128)(2,1)} %bitcast.461, bf16[64,2,6,64]{3,0,2,1:T(8,128)(2,1)S(1)} %bitcast.481, bf16[64,2,6,64]{3,0,2,1:T(8,128)(2,1)S(1)} %bitcast.479), kind=kOutput, calls=%fused_computation.40 | convolution fusion | flops 1623588096 | bytes 29559808 | tf_op jit(solution)/shard_map/tkgd,skd->kgts/dot_general | solution.py:44
  324.6 22.1 %all_gather.59 = bf16[512,2,128]{2,0,1:T(8,128)(2,1)S(1)} all-gather(bf16[64,2,128]{2,0,1:T(8,128)(2,1)S(1)} %convolution_convert_fusion.1), channel_id=1, replica_groups=mesh['req'=2,'cp'=8] {'cp'}, dimensions={0}, use_global_device_ids=true | all-gather | bytes 294912 | tf_op jit(solution)/shard_map/all_gather | solution.py:83
  346.8 11.8 %fusion.186 = f32[64,2,6,128]{3,0,2,1:T(8,128)S(1)} fusion(bf16[8192,2,128,1]{0,2,3,1:T(8,128)(2,1)} %bitcast.493, f32[2,64,6,8192]{3,1,2,0:T(8,128)} %get-tuple-element.66, f32[2,6,64]{2,1,0:T(8,128)S(1)} %add.256, f32[2,6,64]{2,1,0:T(8,128)S(1)} %max.30), kind=kOutput, calls=%fused_computation.146 | convolution fusion | flops 1635778560 | bytes 29759488 | tf_op jit(solution)/shard_map/kgts,skd->tkgd/dot_general | solution.py:53
  362.5 12.4 %fusion.10 = f32[64,8960]{1,0:T(8,128)} fusion(bf16[4,1536,8960]{2,1,0:T(8,128)(2,1)} %param.21, f32[64,1536]{1,0:T(8,128)S(1)} %get-tuple-element.70, f32[1536]{0:T(1024)S(1)} %copy-done.23, f32[64]{0:T(128)S(1)} %add_rsqrt_fusion.2), kind=kOutput, calls=%fused_computation.10 | convolution fusion | flops 1761902592 | bytes 30218496 | tf_op jit(solution)/shard_map/dot_general | solution.py:90
  374.9 21.3 %multiply_reduce_fusion.1 = (f32[64]{0:T(128)S(1)}, f32[64,1536]{1,0:T(8,128)S(1)}) fusion(f32[64,1536]{1,0:T(8,128)S(1)} %get-tuple-element.70, bf16[4,8960,1536]{2,1,0:T(8,128)(2,1)} %param.23, bf16[4,1536,8960]{2,1,0:T(8,128)(2,1)} %param.22, f32[64,8960]{1,0:T(8,128)} %fusion.10, f32[1536]{0:T(1024)S(1)} %copy-done.23, f32[64]{0:T(128)S(1)} %add_rsqrt_fusion.2), kind=kOutput, calls=%fused_computation.181 | convolution fusion | flops 3527442432 | bytes 58532608 | tf_op jit(solution)/shard_map/dot_general | solution.py:93
  408.4 18.2 %all_gather.61 = bf16[512,2,128]{2,0,1:T(8,128)(2,1)S(1)} all-gather(bf16[64,2,128]{2,0,1:T(8,128)(2,1)S(1)} %maximum_convert_fusion.3), channel_id=1, replica_groups=mesh['req'=2,'cp'=8] {'cp'}, dimensions={0}, use_global_device_ids=true | all-gather | bytes 294912 | tf_op jit(solution)/shard_map/all_gather | solution.py:82
  430.7 12.5 %bitcast_reduce_fusion = (f32[2,6,64]{2,1,0:T(8,128)S(1)}, f32[2,64,6,8192]{3,1,2,0:T(8,128)}) fusion(bf16[8192,2,128,1]{0,2,3,1:T(8,128)(2,1)} %bitcast.460, bf16[64,2,6,64]{3,0,2,1:T(8,128)(2,1)S(1)} %bitcast.473, bf16[64,2,6,64]{3,0,2,1:T(8,128)(2,1)S(1)} %bitcast.471), kind=kOutput, calls=%fused_computation.37 | convolution fusion | flops 1623588096 | bytes 29559808 | tf_op jit(solution)/shard_map/tkgd,skd->kgts/dot_general | solution.py:44
  454.6 21.6 %all_gather.63 = bf16[512,2,128]{2,0,1:T(8,128)(2,1)S(1)} all-gather(bf16[64,2,128]{2,0,1:T(8,128)(2,1)S(1)} %convolution_convert_fusion), channel_id=1, replica_groups=mesh['req'=2,'cp'=8] {'cp'}, dimensions={0}, use_global_device_ids=true | all-gather | bytes 294912 | tf_op jit(solution)/shard_map/all_gather | solution.py:83
  476.2 11.8 %fusion.185 = f32[64,2,6,128]{3,0,2,1:T(8,128)S(1)} fusion(bf16[8192,2,128,1]{0,2,3,1:T(8,128)(2,1)} %bitcast.492, f32[2,64,6,8192]{3,1,2,0:T(8,128)} %get-tuple-element.74, f32[2,6,64]{2,1,0:T(8,128)S(1)} %add.265, f32[2,6,64]{2,1,0:T(8,128)S(1)} %max.31), kind=kOutput, calls=%fused_computation.145 | convolution fusion | flops 1635778560 | bytes 29759488 | tf_op jit(solution)/shard_map/kgts,skd->tkgd/dot_general | solution.py:53
  491.9 12.4 %fusion.4 = f32[64,8960]{1,0:T(8,128)} fusion(bf16[4,1536,8960]{2,1,0:T(8,128)(2,1)} %param.21, f32[64,1536]{1,0:T(8,128)S(1)} %get-tuple-element.78, f32[1536]{0:T(1024)S(1)} %copy-done.22, f32[64]{0:T(128)S(1)} %add_rsqrt_fusion), kind=kOutput, calls=%fused_computation.4 | convolution fusion | flops 1761902592 | bytes 30218496 | tf_op jit(solution)/shard_map/dot_general | solution.py:90
  504.3 21.7 %fusion.156 = bf16[64,1536]{1,0:T(8,128)(2,1)} fusion(f32[64,1536]{1,0:T(8,128)S(1)} %get-tuple-element.78, bf16[4,8960,1536]{2,1,0:T(8,128)(2,1)} %param.23, bf16[4,1536,8960]{2,1,0:T(8,128)(2,1)} %param.22, f32[64,8960]{1,0:T(8,128)} %fusion.4, f32[1536]{0:T(1024)S(1)} %copy-done.22, f32[64]{0:T(128)S(1)} %add_rsqrt_fusion), kind=kOutput, calls=%fused_computation.112 | convolution fusion | flops 3527147520 | bytes 58335744 | tf_op jit(solution)/shard_map/dot_general | solution.py:93
  (203 shorter events, 139.4 us)
Async XLA Ops:
  7.2 69.8 %all-gather.17.cloned.1.call-start = ((), (), s32[]{:S(2)}) async-start(), calls=%async_computation.2 | async-start | bytes 4718592 | tf_op jit(solution)/shard_map/all_gather | solution.py:84
  10.4 90.8 %all-gather.19.cloned.1.call-start = ((), (), s32[]{:S(2)}) async-start(), calls=%async_computation.3 | async-start | bytes 4718592 | tf_op jit(solution)/shard_map/all_gather | solution.py:85
  11.9 165.5 %all-gather.21.cloned.1.call-start = ((), (), s32[]{:S(2)}) async-start(), calls=%async_computation.4 | async-start | bytes 4718592 | tf_op jit(solution)/shard_map/all_gather | solution.py:84
  12.7 212.5 %all-gather.23.cloned.1.call-start = ((), (), s32[]{:S(2)}) async-start(), calls=%async_computation.5 | async-start | bytes 4718592 | tf_op jit(solution)/shard_map/all_gather | solution.py:85
  13.3 287.1 %all-gather.25.cloned.1.call-start = ((), (), s32[]{:S(2)}) async-start(), calls=%async_computation.6 | async-start | bytes 4718592 | tf_op jit(solution)/shard_map/all_gather | solution.py:84
  14.0 332.8 %all-gather.27.cloned.1.call-start = ((), (), s32[]{:S(2)}) async-start(), calls=%async_computation.7 | async-start | bytes 4718592 | tf_op jit(solution)/shard_map/all_gather | solution.py:85
  14.6 416.1 %all-gather.29.cloned.1.call-start = ((), (), s32[]{:S(2)}) async-start(), calls=%async_computation.8 | async-start | bytes 4718592 | tf_op jit(solution)/shard_map/all_gather | solution.py:84
  15.4 460.8 %all-gather.31.cloned.1.call-start = ((), (), s32[]{:S(2)}) async-start(), calls=%async_computation.9 | async-start | bytes 4718592 | tf_op jit(solution)/shard_map/all_gather | solution.py:85
  20.2 26.7 %copy-start.12 = (bf16[64,1536]{1,0:T(8,128)(2,1)S(1)}, bf16[64,1536]{1,0:T(8,128)(2,1)}, u32[]{:S(2)}) copy-start(bf16[64,1536]{1,0:T(8,128)(2,1)} %param.12) | copy-start | bytes 589828
  46.9 27.7 %copy-start.19 = (bf16[4,1536]{1,0:T(4,128)(2,1)S(1)}, bf16[4,1536]{1,0:T(4,128)(2,1)}, u32[]{:S(2)}) copy-start(bf16[4,1536]{1,0:T(4,128)(2,1)} %param.16) | copy-start | bytes 36868
  190.4 10.9 %copy-start.8 = (bf16[1,1536,2,128]{3,2,1,0:T(2,128)(2,1)S(1)}, bf16[1,1536,2,128]{3,2,1,0:T(2,128)(2,1)}, u32[]{:S(2)}) copy-start(bf16[1,1536,2,128]{3,2,1,0:T(2,128)(2,1)} %get-tuple-element.13) | copy-start | bytes 2359300
  201.6 35.5 %copy-start.14 = (bf16[64,2,128]{2,0,1:T(8,128)(2,1)}, bf16[64,2,128]{2,0,1:T(8,128)(2,1)S(1)}, u32[]{:S(2)}) copy-start(bf16[64,2,128]{2,0,1:T(8,128)(2,1)S(1)} %convolution_convert_fusion.2) | copy-start | bytes 98308
  253.3 21.2 %copy-start.21 = (f32[1536]{0:T(1024)S(1)}, f32[1536]{0:T(1024)}, u32[]{:S(2)}) copy-start(f32[1536]{0:T(1024)} %get-tuple-element.10) | copy-start | bytes 18436
  313.5 10.9 %copy-start.6 = (bf16[1,1536,2,128]{3,2,1,0:T(2,128)(2,1)S(1)}, bf16[1,1536,2,128]{3,2,1,0:T(2,128)(2,1)}, u32[]{:S(2)}) copy-start(bf16[1,1536,2,128]{3,2,1,0:T(2,128)(2,1)} %get-tuple-element.12) | copy-start | bytes 2359300
  374.9 21.4 %copy-start.15 = (bf16[64,2,128]{2,0,1:T(8,128)(2,1)S(1)}, bf16[64,2,128]{2,0,1:T(8,128)(2,1)}, u32[]{:S(2)}) copy-start(bf16[64,2,128]{2,0,1:T(8,128)(2,1)} %copy-done.14) | copy-start | bytes 98308
  374.9 21.5 %copy-start.10 = (bf16[64,2,128]{2,0,1:T(8,128)(2,1)S(1)}, bf16[64,2,128]{2,0,1:T(8,128)(2,1)}, u32[]{:S(2)}) copy-start(bf16[64,2,128]{2,0,1:T(8,128)(2,1)} %copy-done.9) | copy-start | bytes 98308
  374.9 21.5 %copy-start.20 = (f32[1536]{0:T(1024)S(1)}, f32[1536]{0:T(1024)}, u32[]{:S(2)}) copy-start(f32[1536]{0:T(1024)} %get-tuple-element.7) | copy-start | bytes 18436
  374.9 21.6 %copy-start.4 = (bf16[1,1536,2,128]{3,2,1,0:T(2,128)(2,1)S(1)}, bf16[1,1536,2,128]{3,2,1,0:T(2,128)(2,1)}, u32[]{:S(2)}) copy-start(bf16[1,1536,2,128]{3,2,1,0:T(2,128)(2,1)} %get-tuple-element.11) | copy-start | bytes 2359300
  374.9 22.1 %copy-start.17 = (bf16[1,64,256]{2,1,0:T(8,128)(2,1)S(1)}, bf16[1,64,256]{2,1,0:T(8,128)(2,1)}, u32[]{:S(2)}) copy-start(bf16[1,64,256]{2,1,0:T(8,128)(2,1)} %stack_reshape.16) | copy-start | bytes 98308
  374.9 32.9 %copy-start.5 = (bf16[1,1536,2,128]{3,2,1,0:T(2,128)(2,1)S(1)}, bf16[1,1536,2,128]{3,2,1,0:T(2,128)(2,1)}, u32[]{:S(2)}) copy-start(bf16[1,1536,2,128]{3,2,1,0:T(2,128)(2,1)} %get-tuple-element.15) | copy-start | bytes 2359300
  398.1 129.1 %all-to-all-start.1 = ((bf16[8,2,4096]{2,1,0:T(2,128)(2,1)}), bf16[8,2,4096]{2,1,0:T(2,128)(2,1)S(1)}, u32[]{:S(2)}, u32[]{:S(2)}) async-start(bf16[8,2,4096]{2,1,0:T(2,128)(2,1)} %reshape.431), calls=%async_computation.1 | async-start | bytes 262144 | tf_op jit(solution)/shard_map/all_to_all | solution.py:97
  504.3 21.7 %copy-start.16 = (bf16[1,64,256]{2,1,0:T(8,128)(2,1)S(1)}, bf16[1,64,256]{2,1,0:T(8,128)(2,1)}, u32[]{:S(2)}) copy-start(bf16[1,64,256]{2,1,0:T(8,128)(2,1)} %convert_element_type.272) | copy-start | bytes 98308
  526.1 17.4 %copy-start.1 = (bf16[4,8192,32]{1,2,0:T(8,128)(2,1)S(1)}, bf16[4,8192,32]{1,2,0:T(8,128)(2,1)}, u32[]{:S(2)}) copy-start(bf16[4,8192,32]{1,2,0:T(8,128)(2,1)} %param.14) | copy-start | bytes 6291460
  527.2 17.8 %all-to-all-start = ((bf16[8,2,4096]{2,1,0:T(2,128)(2,1)}), bf16[8,2,4096]{2,1,0:T(2,128)(2,1)S(1)}, u32[]{:S(2)}, u32[]{:S(2)}) async-start(bf16[8,2,4096]{2,1,0:T(2,128)(2,1)} %reshape.429), calls=%async_computation | async-start | bytes 262144 | tf_op jit(solution)/shard_map/all_to_all | solution.py:96
  (11 other events, 42.5 us)
Sparse Core Ops, SparseCore 0:
  10.5 32.0 all-gather.16
  44.2 29.0 all-gather.18
  74.9 27.6 all-gather.20
  104.1 27.6 all-gather.22
  133.2 27.6 all-gather.24
  162.4 28.5 all-gather.26
  192.5 28.0 all-gather.28
  222.3 27.6 all-gather.30
where the time goes:
time: 568 us; the launch traced here: 560 us
  matrix products  265 us (47%)
  blocking collectives  173 us (30%)
  other arithmetic  54.9 us (10%)
  local copies, waits for them, and re-layouts  27.2 us (5%)
  starting transfers between devices  20.4 us (4%)
  between operations  15.5 us (3%)
    all_gather x4, blocking collectives, device_fn(): values_new = lax.all_gather(values_loc, 'cp', axis=0, tiled=True)  89 us
    dot_general x4, matrix products, device_fn(): jnp.dot(gated_act, w_down[layer_idx], preferred_element_type=jnp.float32)  85.3 us
    all_gather x4, blocking collectives, device_fn(): keys_new = lax.all_gather(keys_loc, 'cp', axis=0, tiled=True)  83.9 us
    dot_general x4, matrix products, local_attention(): jnp.einsum('tkgd,skd->kgts', queries, keys_pre, preferred_element_type=jn...  50.1 us
    dot_general x4, matrix products, device_fn(): jnp.dot(normed_mlp, w_gate[layer_idx], preferred_element_type=jnp.float32)  49.5 us
    dot_general x4, matrix products, local_attention(): jnp.einsum('kgts,skd->tkgd', probs_pre, values_pre, preferred_element_typ...  47.3 us
    reduce_sum x8, other arithmetic, local_attention(): denominator = (exp_pre.sum(axis=-1) + exp_new.sum(axis=-1))[..., None]  45.7 us
    dot_general x4, matrix products, device_fn(): jnp.einsum('the,hed->td', attn_out, w_out[layer_idx], preferred_element_t...  13.5 us
  transfers between devices with their start and end apart: 10, of which 0 were waited for; matrix products, arithmetic and copies ran while one was open for 60% of the time, Pallas kernels for 0%

commit v1 on v0

v1 whole, which is shorter than its diff:
```python
import functools
import math

import jax
import jax.numpy as jnp
from jax import lax
from jax.experimental import pallas as pl
from jax.experimental.pallas import tpu as pltpu
from jax.sharding import PartitionSpec as P

NORM_EPS = 1e-5
ROPE_THETA = 500000.0
MESH = pl.DeviceIdType.MESH
F32 = jnp.float32
BF16 = jnp.bfloat16

COMM_CHUNK = 2048
KEY_CHUNK = 1024
FF_CHUNK = 640
SLOTS = 4


def rms(x, gain):
    xf = x.astype(F32)
    inv = lax.rsqrt(jnp.mean(xf * xf, axis=-1, keepdims=True) + NORM_EPS)
    return (xf * inv * gain.astype(F32)).astype(BF16)


def mm(a, b):
    return jnp.dot(a, b, preferred_element_type=F32)


def mm_t(a, b):
    return lax.dot_general(a, b, (((1,), (1,)), ((), ())), preferred_element_type=F32)


def kernel(cfg, x_in, pk, pv, g1, g2, wq, wkv, wo, wg, wu, wd, cos_ref, sin_ref,
           x_out, k_out, v_out,
           kv, gu, w2, wq_v, wkv_v, wo_v, nkv, kvs, qs, qr, h2, acc, part, x_s, att_own, att_snd, att_rcv,
           m_s, l_s, o_s, tr,
           lsem, ss_sib, ss_nbr, ss_fwd, rs_sib, rs_nbr, rs_fwd, nk_s, nk_r, q_sem, o_sem, h_sem, p_sem,
           wq_sem, wkv_sem, wo_sem, gu_sem, w2_sem):
    n, L, D, heads, kvh, hd, tok, cols, plen = cfg
    grp = heads // kvh
    per = n // kvh
    grows = grp * tok
    gcols = grp * hd
    nch = plen // COMM_CHUNK
    ff_half = wg.shape[2] // 2
    nff = ff_half // FF_CHUNK
    total_ff = L * nff
    scale = hd ** -0.5 * math.log2(math.e)

    me = lax.axis_index('cp')
    core = lax.rem(me, 2)
    chip = lax.div(me, 2)
    kvj = lax.div(me, per)
    quarter = lax.rem(me, per)
    sib = me + 1 - 2 * core
    nbr = kvj * per + lax.rem(quarter + 2, per)
    mate = 2 * (n // 2 - 1 - chip) + core

    def rows_of(dev):
        return pl.ds(pl.multiple_of(lax.rem(dev, per) * cols, cols), cols)

    my_rows = rows_of(me)
    nbr_rows = rows_of(nbr)
    sib_rows = rows_of(sib)
    sibnbr = kvj * per + lax.rem(lax.rem(sib, per) + 2, per)
    sibnbr_rows = rows_of(sibnbr)

    def rcopy(src, dst, s, r, dev):
        return pltpu.make_async_remote_copy(src_ref=src, dst_ref=dst, send_sem=s, recv_sem=r,
                                            device_id={'cp': dev}, device_id_type=MESH)

    def cpos(ch):
        return pl.ds(ch * COMM_CHUNK if isinstance(ch, int) else pl.multiple_of(ch * COMM_CHUNK, COMM_CHUNK), COMM_CHUNK)

    def wq_start(l):
        for h in range(heads):
            pltpu.make_async_copy(wq.at[l, h], wq_v.at[:, pl.ds(h * hd, hd)], wq_sem).start()
        pltpu.make_async_copy(wkv.at[l], wkv_v, wkv_sem).start()

    def wo_start(l):
        pltpu.make_async_copy(wo.at[l], wo_v, wo_sem).start()

    def ff_copies(g):
        l = lax.div(g, nff)
        off = pl.multiple_of(core * ff_half + lax.rem(g, nff) * FF_CHUNK, 128)
        slot = lax.rem(g, SLOTS)
        return (pltpu.make_async_copy(wg.at[l, :, pl.ds(off, FF_CHUNK)], gu.at[slot, :, pl.ds(0, FF_CHUNK)], gu_sem.at[slot, 0]),
                pltpu.make_async_copy(wu.at[l, :, pl.ds(off, FF_CHUNK)], gu.at[slot, :, pl.ds(FF_CHUNK, FF_CHUNK)], gu_sem.at[slot, 1]),
                pltpu.make_async_copy(wd.at[l, pl.ds(off, FF_CHUNK), :], w2.at[slot], w2_sem.at[slot]))

    def ff_start(g):
        for c in ff_copies(g):
            c.start()

    def own_local(l):
        pltpu.make_async_copy(pk.at[l], kv.at[l, 0, my_rows, :], lsem.at[l]).start()
        pltpu.make_async_copy(pv.at[l], kv.at[l, 1, my_rows, :], lsem.at[l]).start()

    def own_send(l):
        def body(ch, _):
            for i, src in enumerate((pk, pv)):
                rcopy(src.at[l, :, cpos(ch)], kv.at[l, i, my_rows, cpos(ch)], ss_nbr.at[l], rs_nbr.at[l, ch], nbr).start()
                rcopy(src.at[l, :, cpos(ch)], kv.at[l, i, my_rows, cpos(ch)], ss_sib.at[l], rs_sib.at[l, ch], sib).start()
            return 0
        lax.fori_loop(0, nch, body, 0)

    def forward(l, ch):
        blk = kv.at[l, :, nbr_rows, cpos(ch)]
        rcopy(blk, blk, ss_nbr.at[l], rs_nbr.at[l, ch], nbr).wait_recv()
        rcopy(blk, blk, ss_fwd.at[l], rs_fwd.at[l, ch], sib).start()

    def chunk_ready(l, ch):
        @pl.when(ch + 1 < nch)
        def _():
            forward(l, ch + 1)
        blk = kv.at[l, :, sib_rows, cpos(ch)]
        rcopy(blk, blk, ss_sib.at[l], rs_sib.at[l, ch], sib).wait_recv()
        blk = kv.at[l, :, sibnbr_rows, cpos(ch)]
        rcopy(blk, blk, ss_fwd.at[l], rs_fwd.at[l, ch], sib).wait_recv()

    barrier = pltpu.get_barrier_semaphore()
    for off in range(1, n):
        pl.semaphore_signal(barrier, inc=1, device_id={'cp': lax.rem(me + off, n)}, device_id_type=MESH)

    wq_start(0)
    own_local(0)
    wo_start(0)
    x_s[...] = x_in[...]
    pl.semaphore_wait(barrier, n - 1)
    own_send(0)

    def prime(g, _):
        ff_start(g)
        return 0
    lax.fori_loop(0, SLOTS, prime, 0)

    def local_rest(l, _):
        own_local(l)
        return 0
    lax.fori_loop(1, L, local_rest, 0)

    def token_pos(t, dev):
        half = tok // 2
        return jnp.where(t < half, dev * half + t, (2 * n - 1 - dev) * half + t - half)

    def reset(st):
        m_s[st] = jnp.full((grows, hd), -jnp.inf, F32)
        l_s[st] = jnp.zeros((grows, hd), F32)
        o_s[st] = jnp.zeros((grows, hd), F32)

    def fold(st, s, pv_dot):
        width = s.shape[1]
        m_prev = m_s[st]
        m_new = jnp.maximum(m_prev, jnp.max(s, axis=1, keepdims=True))
        alpha = jnp.exp2((m_prev - m_new) * scale)
        p = jnp.exp2((s - jnp.concatenate([m_new] * (width // hd), axis=1)) * scale)
        lsum = p[:, :hd]
        for b in range(1, width // hd):
            lsum = lsum + p[:, b * hd:(b + 1) * hd]
        m_s[st] = m_new
        l_s[st] = alpha * l_s[st] + lsum
        o_s[st] = alpha * o_s[st] + pv_dot(p.astype(BF16))

    def attend_prefix(l, st, q_at, ch):
        for sub in range(COMM_CHUNK // KEY_CHUNK):
            pos = pl.ds(pl.multiple_of(ch * COMM_CHUNK + sub * KEY_CHUNK, KEY_CHUNK), KEY_CHUNK)
            s = mm(q_at(), kv[l, 0, :, pos])
            fold(st, s, lambda p: mm_t(p, kv[l, 1, :, pos]))

    def attend_new(l, st, q_at, dev):
        s = mm_t(q_at(), nkv[l, 0])
        width = n * tok
        tq = lax.broadcasted_iota(jnp.int32, (grows, width), 0) & (tok - 1)
        col = lax.broadcasted_iota(jnp.int32, (grows, width), 1)
        tk = col & (tok - 1)
        dk = col >> (tok.bit_length() - 1)
        allowed = token_pos(tk, dk) <= token_pos(tq, dev)
        s = jnp.where(allowed, s, -jnp.inf)
        fold(st, s, lambda p: mm(p, nkv[l, 1]))

    def finish(st, dst):
        o = (o_s[st] / jnp.sum(l_s[st], axis=1, keepdims=True)).astype(BF16)
        for h in range(grp):
            dst[:, h * hd:(h + 1) * hd] = o[h * tok:(h + 1) * tok, :]

    own_q = pl.ds(pl.multiple_of(kvj * grows, grows), grows)
    mate_q = pl.ds(pl.multiple_of((1 - kvj) * grows, grows), grows)
    own_tok = pl.ds(pl.multiple_of(core * tok, tok), tok)
    sib_tok = pl.ds(pl.multiple_of((1 - core) * tok, tok), tok)
    my_new = pl.ds(pl.multiple_of(me * tok, tok), tok)

    def layer(l, _):
        @pl.when(l > 0)
        def _():
            forward(l, 0)
        h = rms(x_s[...], g1[l])
        pltpu.make_async_copy(wo.at[l], wq_v, wq_sem).wait()
        cos_t = cos_ref[...]
        sin_t = sin_ref[...]

        def rope(z):
            return (z * cos_t + pltpu.roll(z, hd // 2, 1) * sin_t).astype(BF16)

        for pr in range(heads // 2):
            y = mm(h, wq_v[:, 2 * pr * hd:(2 * pr + 2) * hd])
            for s in range(2):
                hh = 2 * pr + s
                qs[hh * tok:(hh + 1) * tok, :] = rope(y[:, s * hd:(s + 1) * hd])
        q_copy = rcopy(qs.at[mate_q, :], qr, q_sem.at[0], q_sem.at[1], mate)
        q_copy.start()
        pltpu.make_async_copy(wkv.at[l], wkv_v, wkv_sem).wait()
        for i in range(2):
            y = mm(h, wkv_v[:, i * kvh * hd:(i + 1) * kvh * hd])
            for j in range(kvh):
                z = y[:, j * hd:(j + 1) * hd]
                kvs[j, i] = rope(z) if i == 0 else z.astype(BF16)

        @pl.when(l + 1 < L)
        def _():
            wq_start(l + 1)

        for i in range(2):
            nkv[l, i, my_new, :] = kvs[kvj, i]

        def nk_copy(off):
            dst = lax.rem(me + off, n)
            return rcopy(kvs.at[lax.div(dst, per)], nkv.at[l, :, my_new, :], nk_s.at[off], nk_r.at[l, me], dst)

        for off in range(1, n):
            nk_copy(off).start()

        @pl.when(l + 1 < L)
        def _():
            own_send(l + 1)

        @pl.when(l == 0)
        def _():
            forward(l, 0)
        full = kv.at[l, :, my_rows, :]
        pltpu.make_async_copy(full, full, lsem.at[l]).wait()

        reset(0)
        reset(1)

        def own_chunk(ch, _):
            attend_prefix(l, 0, lambda: qs[own_q, :], ch)
            return 0

        def first_half(ch, _):
            chunk_ready(l, ch)
            return own_chunk(ch, 0)
        lax.fori_loop(0, nch // 2, first_half, 0)
        q_copy.wait_recv()

        def mate_chunk(ch, _):
            @pl.when(ch >= nch // 2)
            def _():
                chunk_ready(l, ch)
            attend_prefix(l, 1, lambda: qr[...], ch)
            return 0
        lax.fori_loop(0, nch, mate_chunk, 0)
        for off in range(1, n):
            src = lax.rem(me + off, n)
            blk = nkv.at[l, :, pl.ds(pl.multiple_of(src * tok, tok), tok), :]
            rcopy(blk, blk, nk_s.at[off], nk_r.at[l, src], src).wait_recv()
        attend_new(l, 1, lambda: qr[...], mate)
        finish(1, att_snd)
        o_copy = rcopy(att_snd, att_rcv, o_sem.at[0], o_sem.at[1], mate)
        o_copy.start()
        lax.fori_loop(nch // 2, nch, own_chunk, 0)
        attend_new(l, 0, lambda: qs[own_q, :], me)
        finish(0, att_own)

        pltpu.make_async_copy(wo.at[l], wo_v, wo_sem).wait()
        y = mm(att_own[...], wo_v[pl.ds(pl.multiple_of(kvj * gcols, gcols), gcols), :])
        o_copy.wait_recv()
        y = y + mm(att_rcv[...], wo_v[pl.ds(pl.multiple_of((1 - kvj) * gcols, gcols), gcols), :])
        x1 = (x_s[...].astype(F32) + y).astype(BF16)
        x_s[...] = x1
        h2[own_tok, :] = rms(x1, g2[l])
        h_copy = rcopy(h2.at[own_tok, :], h2.at[own_tok, :], h_sem.at[0], h_sem.at[1], sib)
        h_copy.start()

        @pl.when(l + 1 < L)
        def _():
            wo_start(l + 1)
        q_copy.wait_send()
        o_copy.wait_send()
        for off in range(1, n):
            nk_copy(off).wait_send()
        half = tok // 2
        for i, out in enumerate((k_out, v_out)):
            pieces = [nkv[l, i, d * tok:d * tok + half, :] for d in range(n)]
            pieces += [nkv[l, i, d * tok + half:(d + 1) * tok, :] for d in reversed(range(n))]
            tr[...] = jnp.concatenate(pieces, axis=0).astype(F32).T
            out[l] = tr[my_rows, :].astype(BF16)
        h_copy.wait_recv()

        acc[...] = jnp.zeros_like(acc)

        def ff(i, _):
            g = l * nff + i
            slot = lax.rem(g, SLOTS)
            cg, cu, cd = ff_copies(g)
            cg.wait()
            cu.wait()
            y = mm(h2[...], gu[slot])
            gate = y[:, :FF_CHUNK]
            act = (gate * jax.nn.sigmoid(gate) * y[:, FF_CHUNK:]).astype(BF16)
            cd.wait()
            acc[...] += mm(act, w2[slot])

            @pl.when(g + SLOTS < total_ff)
            def _():
                ff_start(g + SLOTS)
            return 0
        lax.fori_loop(0, nff, ff, 0)
        p_copy = rcopy(acc.at[sib_tok, :], part, p_sem.at[0], p_sem.at[1], sib)
        p_copy.start()
        h_copy.wait_send()
        mine = x_s[...].astype(F32) + acc[own_tok, :]
        p_copy.wait_recv()
        x_s[...] = (mine + part[...]).astype(BF16)
        p_copy.wait_send()
        return 0

    lax.fori_loop(0, L, layer, 0)
    x_out[...] = x_s[...]

    def drain(l, _):
        full = kv.at[l, :, my_rows, :]
        rcopy(full, full, ss_sib.at[l], rs_sib.at[l, 0], sib).wait_send()
        rcopy(full, full, ss_nbr.at[l], rs_nbr.at[l, 0], nbr).wait_send()
        full = kv.at[l, :, nbr_rows, :]
        rcopy(full, full, ss_fwd.at[l], rs_fwd.at[l, 0], sib).wait_send()
        return 0
    lax.fori_loop(0, L, drain, 0)


def solution(mesh):
    n = mesh.shape['cp']

    def device_fn(hidden, prefix_k, prefix_v, gain_attn, gain_mlp, w_query, w_key, w_value, w_out, w_gate, w_up, w_down):
        L, D, kvh, hd = w_key.shape
        heads = w_query.shape[2]
        tok = hidden.shape[0]
        plen = prefix_k.shape[1]
        cols = prefix_k.shape[2]
        ff = w_gate.shape[2]
        grp = heads // kvh
        half = tok // 2
        me = lax.axis_index('cp')
        pieces = jnp.stack([me, 2 * n - 1 - me])
        pos = (plen + pieces[:, None] * half + jnp.arange(half)).reshape(-1)
        inv_freq = ROPE_THETA ** (-jnp.arange(0, hd, 2, dtype=F32) / hd)
        ang = pos.astype(F32)[:, None] * inv_freq[None, :]
        cos_t = jnp.cos(ang)
        sin_t = jnp.sin(ang)
        cos2 = jnp.concatenate([cos_t, cos_t], axis=1)
        sin2 = jnp.concatenate([-sin_t, sin_t], axis=1)
        pk = prefix_k.transpose(0, 2, 1)
        pv = prefix_v.transpose(0, 2, 1)
        wq = w_query.transpose(0, 2, 1, 3)
        wkv = jnp.concatenate([w_key.reshape(L, D, kvh * hd), w_value.reshape(L, D, kvh * hd)], axis=2)
        wo = w_out.reshape(L, heads * hd, D)
        g1 = gain_attn[:, None, :]
        g2 = gain_mlp[:, None, :]
        cfg = (n, L, D, heads, kvh, hd, tok, cols, plen)
        nch = plen // COMM_CHUNK
        rows = grp * tok
        dma = pltpu.SemaphoreType.DMA
        vm = pl.BlockSpec(memory_space=pltpu.VMEM)
        hbm = pl.BlockSpec(memory_space=pl.ANY)
        hid, nk, nv = pl.pallas_call(
            functools.partial(kernel, cfg),
            out_shape=(jax.ShapeDtypeStruct((tok, D), BF16),
                       jax.ShapeDtypeStruct((L, cols, n * tok), BF16),
                       jax.ShapeDtypeStruct((L, cols, n * tok), BF16)),
            in_specs=[vm, hbm, hbm, vm, vm, hbm, hbm, hbm, hbm, hbm, hbm, vm, vm],
            out_specs=(vm, vm, vm),
            scratch_shapes=[
                pltpu.VMEM((L, 2, hd, plen), BF16),
                pltpu.VMEM((SLOTS, D, 2 * FF_CHUNK), BF16),
                pltpu.VMEM((SLOTS, FF_CHUNK, D), BF16),
                pltpu.VMEM((D, heads * hd), BF16),
                pltpu.VMEM((D, 2 * kvh * hd), BF16),
                pltpu.VMEM((heads * hd, D), BF16),
                pltpu.VMEM((L, 2, n * tok, hd), BF16),
                pltpu.VMEM((kvh, 2, tok, hd), BF16),
                pltpu.VMEM((heads * tok, hd), BF16),
                pltpu.VMEM((rows, hd), BF16),
                pltpu.VMEM((2 * tok, D), BF16),
                pltpu.VMEM((2 * tok, D), F32),
                pltpu.VMEM((tok, D), F32),
                pltpu.VMEM((tok, D), BF16),
                pltpu.VMEM((tok, grp * hd), BF16),
                pltpu.VMEM((tok, grp * hd), BF16),
                pltpu.VMEM((tok, grp * hd), BF16),
                pltpu.VMEM((2, rows, hd), F32),
                pltpu.VMEM((2, rows, hd), F32),
                pltpu.VMEM((2, rows, hd), F32),
                pltpu.VMEM((hd, n * tok), F32),
                dma((L,)), dma((L,)), dma((L,)), dma((L,)),
                dma((L, nch)), dma((L, nch)), dma((L, nch)),
                dma((n,)), dma((L, n)),
                dma((2,)), dma((2,)), dma((2,)), dma((2,)),
                dma, dma, dma, dma((SLOTS, 2)), dma((SLOTS,)),
            ],
            compiler_params=pltpu.CompilerParams(collective_id=0, has_side_effects=True, vmem_limit_bytes=67043328),
            name='prefill',
        )(hidden, pk, pv, g1, g2, wq, wkv, wo, w_gate, w_up, w_down, cos2, sin2)
        cache_k = jnp.concatenate([pk, nk], axis=2).transpose(0, 2, 1)
        cache_v = jnp.concatenate([pv, nv], axis=2).transpose(0, 2, 1)
        return hid, cache_k, cache_v

    in_specs = (P(('req', 'cp'), None), P(None, 'req', 'cp'), P(None, 'req', 'cp')) + (P(),) * 9
    out_specs = (P(('req', 'cp'), None), P(None, 'req', 'cp'), P(None, 'req', 'cp'))
    return jax.shard_map(device_fn, mesh=mesh, in_specs=in_specs, out_specs=out_specs, check_vma=False)
```

time: 568 us -> 172 us (0.30); the launches traced: 560 us -> 172 us
  matrix products: 265 us -> 0 us
  blocking collectives: 173 us -> 0 us
  Pallas kernels: 0 us -> 146 us
  other arithmetic: 54.9 us -> 10.9 us
  starting transfers between devices: 20.4 us -> 0 us
  between operations: 15.5 us -> 0.68 us
  local copies, waits for them, and re-layouts: 27.2 us -> 14 us
    dot_general x40 -> x0, matrix products: 265 us -> none  [the longest x4 85.3 us: device_fn(): jnp.dot(gated_act, w_down[layer_idx], preferred_element_type=jnp.float32)]
    all_gather x8 -> x0, blocking collectives: 173 us -> none  [the longest x4 89 us: device_fn(): values_new = lax.all_gather(values_loc, 'cp', axis=0, tiled=True)]
    pallas_call x0 -> x1, Pallas kernels: none -> 146 us  [device_fn(): pl.pallas_call(functools.partial(kernel, cfg), out_shape=(jax.ShapeDtypeS...]
    reduce_sum x9 -> x0, other arithmetic: 45.8 us -> none  [the longest x8 45.7 us: local_attention(): denominator = (exp_pre.sum(axis=-1) + exp_new.sum(axis=-1))[..., None]]
    all_to_all x2 -> x0, starting transfers between devices: 19.9 us -> none  [the longest x1 10.2 us: device_fn(): keys_sent = lax.all_to_all(jnp.stack(keys_kept), 'cp', 2, 1, tiled=True)]
    slice x10 -> x0, local copies, waits for them, and re-layouts: 19.1 us -> none  [the longest x4 4.73 us: to_natural(): blocks[:, :, 0]]
    reshape x4 -> x2, local copies, waits for them, and re-layouts: 0.86 us -> 10.6 us  [the longest x1 6.03 us: device_fn(): w_key.reshape(L, D, kvh * hd)]
  transfers between devices with their start and end apart: 10 -> 0, of which waited for: 0 -> 0; matrix products, arithmetic and copies ran while one was open for 60% -> 0% of each run, Pallas kernels for 0% -> 0%
where the time goes in v1:
time: 172 us
  Pallas kernels  146 us (85%)
  local copies, waits for them, and re-layouts  14 us (8%)
  other arithmetic  10.9 us (6%)
    pallas_call x1, Pallas kernels, device_fn(): pl.pallas_call(functools.partial(kernel, cfg), out_shape=(jax.ShapeDtypeS...  146 us
    reshape x1, local copies, waits for them, and re-layouts, device_fn(): w_key.reshape(L, D, kvh * hd)  6.03 us
    concatenate x1, other arithmetic, device_fn(): jnp.concatenate([w_key.reshape(L, D, kvh * hd), w_value.reshape(L, D, kvh...  5.04 us
    reshape x1, local copies, waits for them, and re-layouts, device_fn(): w_value.reshape(L, D, kvh * hd)  4.57 us

profile of v1, /device:TPU:113, one launch (start us, length us, event | category | flops | bytes accessed | tf_op | source)
XLA Modules:
  0.0 171.8 jit_solution(40172065116629652)
XLA Ops:
  0.6 1.3 copy.15.g1
  2.0 1.3 copy.16.g2
  3.3 4.6 %reshape.58 = bf16[4,1536,256]{2,1,0:T(8,128)(2,1)S(1)} reshape(bf16[4,1536,2,128]{3,2,1,0:T(2,128)(2,1)} %param.19) | data formatting | bytes 6291456 | tf_op jit(solution)/shard_map/reshape | solution.py:368
  7.9 6.0 %reshape.57 = bf16[4,1536,256]{2,1,0:T(8,128)(2,1)} reshape(bf16[4,1536,2,128]{3,2,1,0:T(2,128)(2,1)} %param.18) | data formatting | bytes 6291456 | tf_op jit(solution)/shard_map/reshape | solution.py:368
  13.9 5.0 %pad_maximum_fusion.wkv = bf16[4,1536,512]{2,1,0:T(8,128)(2,1)} fusion(bf16[4,1536,256]{2,1,0:T(8,128)(2,1)S(1)} %reshape.58, bf16[4,1536,256]{2,1,0:T(8,128)(2,1)} %reshape.57), kind=kLoop, calls=%fused_computation | loop fusion | flops 12582912 | bytes 12582912 | tf_op jit(solution)/shard_map/concatenate | solution.py:368
  19.0 0.1 fusion.1
  19.0 0.1 add_convert_fusion
  19.1 0.1 convert_element_type.11
  19.2 0.2 fusion
  19.4 0.7 pad_maximum_fusion.1
  20.1 146.1 %prefill.1 = (bf16[64,1536]{1,0:T(8,128)(2,1)}, bf16[4,32,512]{2,1,0:T(8,128)(2,1)}, bf16[4,32,512]{2,1,0:T(8,128)(2,1)}) custom-call(bf16[64,1536]{1,0:T(8,128)(2,1)} %x_in.1, bf16[4,32,8192]{2,1,0:T(8,128)(2,1)} %bitcast.14, bf16[4,32,8192]{2,1,0:T(8,128)(2,1)} %bitcast.16, bf16[4,1,1536]{2,1,0:T(2,128)(2,1)} %copy.15.g1, bf16[4,1,1536]{2,1,0:T(2,128)(2,1)} %copy.16.g2, ...), custom_call_target="tpu_custom_call" | custom-call | tf_op jit(solution)/shard_map/prefill/pallas_call | solution.py:378
  166.2 0.0 copy-start
  166.3 0.0 copy-start.2
  166.3 0.0 copy-start.1
  166.3 3.3 %maximum_bitcast_fusion = bf16[4,8704,32]{1,2,0:T(8,128)(2,1)} fusion(bf16[4,32,512]{2,1,0:T(8,128)(2,1)} %get-tuple-element.7, bf16[4,32,8192]{2,1,0:T(8,128)(2,1)} %bitcast.15), kind=kLoop, calls=%fused_computation.1 | loop fusion | flops 4456448 | bytes 4456448 | tf_op jit(solution)/shard_map/transpose | solution.py:416
  169.6 0.0 copy-done
  169.6 0.0 copy-done.2
  169.6 1.5 maximum_bitcast_fusion.1
  171.1 0.0 copy-done.1
  171.1 0.7 copy.18
  (1 shorter events, 0.0 us)
Async XLA Ops:
  166.2 3.3 %copy-start = (bf16[4,8192,32]{1,2,0:T(8,128)(2,1)S(1)}, bf16[4,8192,32]{1,2,0:T(8,128)(2,1)}, u32[]{:S(2)}) copy-start(bf16[4,8192,32]{1,2,0:T(8,128)(2,1)} %param.14) | copy-start | bytes 6291460
  166.3 3.3 %copy-start.2 = (bf16[4,32,512]{2,1,0:T(8,128)(2,1)S(1)}, bf16[4,32,512]{2,1,0:T(8,128)(2,1)}, u32[]{:S(2)}) copy-start(bf16[4,32,512]{2,1,0:T(8,128)(2,1)} %get-tuple-element.8) | copy-start | bytes 393220
  166.3 4.8 %copy-start.1 = (bf16[64,1536]{1,0:T(8,128)(2,1)S(1)}, bf16[64,1536]{1,0:T(8,128)(2,1)}, u32[]{:S(2)}) copy-start(bf16[64,1536]{1,0:T(8,128)(2,1)} %get-tuple-element.17) | copy-start | bytes 589828

commit v2 on v1

v2 whole, which is shorter than its diff:
```python
import functools
import math

import jax
import jax.numpy as jnp
from jax import lax
from jax.experimental import pallas as pl
from jax.experimental.pallas import tpu as pltpu
from jax.sharding import PartitionSpec as P

NORM_EPS = 1e-5
ROPE_THETA = 500000.0
MESH = pl.DeviceIdType.MESH
F32 = jnp.float32
BF16 = jnp.bfloat16

COMM_CHUNK = 2048
KEY_CHUNK = 1024
GU_CHUNK = 512
GU_SLOTS = 6
DN_CHUNK = 256
DN_SLOTS = 6


def rms(x, gain):
    xf = x.astype(F32)
    inv = lax.rsqrt(jnp.mean(xf * xf, axis=-1, keepdims=True) + NORM_EPS)
    return (xf * inv * gain.astype(F32)).astype(BF16)


def mm(a, b):
    return jnp.dot(a, b, preferred_element_type=F32)


def mm_t(a, b):
    return lax.dot_general(a, b, (((1,), (1,)), ((), ())), preferred_element_type=F32)


def kernel(cfg, x_in, pk, pv, g1, g2, wq, wk, wv, wo, wg, wu, wd, cos_ref, sin_ref,
           x_out, k_out, v_out,
           kv, gu, w2, wq_v, wkv_v, wo_v, nkv, kvs, qs, qr, h2, act, pr, part, x_s, att_own, att_snd, att_rcv,
           m_s, l_s, o_s, tr, gains, gain_v, trig, spread, wide, newc,
           lsem, ss_sib, ss_nbr, ss_fwd, rs_sib, rs_nbr, rs_fwd, nk_s, nk_r, q_sem, o_sem, h_sem, p_send, p_recv,
           wq_sem, wkv_sem, wo_sem, gu_sem, w2_sem, in_sem, new_sem, credit):
    n, L, D, heads, kvh, hd, tok, cols, plen = cfg
    grp = heads // kvh
    per = n // kvh
    grows = grp * tok
    gcols = grp * hd
    nch = plen // COMM_CHUNK
    ff_half = wg.shape[2] // 2
    ngu = pl.cdiv(ff_half, GU_CHUNK)
    ndn = D // DN_CHUNK
    ksplit = ff_half // 2 // 256 * 256 + 256
    scale = hd ** -0.5 * math.log2(math.e)

    me = lax.axis_index('cp')
    core = lax.rem(me, 2)
    chip = lax.div(me, 2)
    kvj = lax.div(me, per)
    quarter = lax.rem(me, per)
    sib = me + 1 - 2 * core
    nbr = kvj * per + lax.rem(quarter + 2, per)
    mate = 2 * (n // 2 - 1 - chip) + core

    def rows_of(dev):
        return pl.ds(pl.multiple_of(lax.rem(dev, per) * cols, cols), cols)

    my_rows = rows_of(me)
    nbr_rows = rows_of(nbr)
    sib_rows = rows_of(sib)
    sibnbr = kvj * per + lax.rem(lax.rem(sib, per) + 2, per)
    sibnbr_rows = rows_of(sibnbr)

    def rcopy(src, dst, s, r, dev):
        return pltpu.make_async_remote_copy(src_ref=src, dst_ref=dst, send_sem=s, recv_sem=r,
                                            device_id={'cp': dev}, device_id_type=MESH)

    def cpos(ch):
        return pl.ds(ch * COMM_CHUNK if isinstance(ch, int) else pl.multiple_of(ch * COMM_CHUNK, COMM_CHUNK), COMM_CHUNK)

    def wq_start(l):
        for h in range(heads):
            pltpu.make_async_copy(wq.at[l, h], wq_v.at[:, pl.ds(h * hd, hd)], wq_sem).start()
        for i, src in enumerate((wk, wv)):
            pltpu.make_async_copy(src.at[l], wkv_v.at[:, pl.ds(i * hd, hd)], wkv_sem.at[i]).start()

    def wo_start(l):
        pltpu.make_async_copy(wo.at[l], wo_v, wo_sem).start()

    def gu_off(i):
        return pl.multiple_of(jnp.minimum(i * GU_CHUNK, ff_half - GU_CHUNK), 128)

    def gu_copies(g):
        l = lax.div(g, ngu)
        off = pl.multiple_of(core * ff_half + gu_off(lax.rem(g, ngu)), 128)
        slot = lax.rem(g, GU_SLOTS)
        return (pltpu.make_async_copy(wg.at[l, :, pl.ds(off, GU_CHUNK)], gu.at[slot, :, pl.ds(0, GU_CHUNK)], gu_sem.at[slot, 0]),
                pltpu.make_async_copy(wu.at[l, :, pl.ds(off, GU_CHUNK)], gu.at[slot, :, pl.ds(GU_CHUNK, GU_CHUNK)], gu_sem.at[slot, 1]))

    def gu_start(g):
        for c in gu_copies(g):
            c.start()

    def gu_wait(g):
        for c in gu_copies(g):
            c.wait()

    def dn_copy(g):
        l = lax.div(g, ndn)
        row = pl.multiple_of(core * ff_half, 128)
        col = pl.multiple_of(lax.rem(g, ndn) * DN_CHUNK, DN_CHUNK)
        slot = lax.rem(g, DN_SLOTS)
        return pltpu.make_async_copy(wd.at[l, pl.ds(row, ff_half), pl.ds(col, DN_CHUNK)], w2.at[slot], w2_sem.at[slot])

    def own_local(l):
        b = lax.rem(l, 2)
        pltpu.make_async_copy(pk.at[l], kv.at[b, 0, my_rows, :], lsem.at[l]).start()
        pltpu.make_async_copy(pv.at[l], kv.at[b, 1, my_rows, :], lsem.at[l]).start()

    def own_send(l):
        b = lax.rem(l, 2)

        def body(ch, _):
            for i, src in enumerate((pk, pv)):
                rcopy(src.at[l, :, cpos(ch)], kv.at[b, i, my_rows, cpos(ch)], ss_nbr.at[l], rs_nbr.at[l, ch], nbr).start()
                rcopy(src.at[l, :, cpos(ch)], kv.at[b, i, my_rows, cpos(ch)], ss_sib.at[l], rs_sib.at[l, ch], sib).start()
            return 0
        lax.fori_loop(0, nch, body, 0)

    def forward(l, ch):
        blk = kv.at[lax.rem(l, 2), :, nbr_rows, cpos(ch)]
        rcopy(blk, blk, ss_nbr.at[l], rs_nbr.at[l, ch], nbr).wait_recv()
        rcopy(blk, blk, ss_fwd.at[l], rs_fwd.at[l, ch], sib).start()

    def chunk_ready(l, ch):
        @pl.when(ch + 1 < nch)
        def _():
            forward(l, ch + 1)
        blk = kv.at[lax.rem(l, 2), :, sib_rows, cpos(ch)]
        rcopy(blk, blk, ss_sib.at[l], rs_sib.at[l, ch], sib).wait_recv()
        blk = kv.at[lax.rem(l, 2), :, sibnbr_rows, cpos(ch)]
        rcopy(blk, blk, ss_fwd.at[l], rs_fwd.at[l, ch], sib).wait_recv()

    def kv_free(l):
        full = kv.at[lax.rem(l, 2), :, nbr_rows, :]
        rcopy(full, full, ss_fwd.at[l], rs_fwd.at[l, 0], sib).wait_send()

        @pl.when(l + 2 < L)
        def _():
            pl.semaphore_signal(credit.at[0], inc=1, device_id={'cp': nbr}, device_id_type=MESH)
            pl.semaphore_signal(credit.at[1], inc=1, device_id={'cp': sib}, device_id_type=MESH)
            own_local(l + 2)

    barrier = pltpu.get_barrier_semaphore()
    for off in range(1, n):
        pl.semaphore_signal(barrier, inc=1, device_id={'cp': lax.rem(me + off, n)}, device_id_type=MESH)

    small = [pltpu.make_async_copy(src, dst, in_sem.at[i]) for i, (src, dst) in enumerate(
        ((x_in, x_s), (g1, gain_v.at[0]), (g2, gain_v.at[1]), (cos_ref, trig.at[0]), (sin_ref, trig.at[1])))]
    for c in small:
        c.start()
    wq_start(0)
    pl.semaphore_wait(barrier, n - 1)
    own_send(0)
    own_local(0)
    wo_start(0)

    def prime_gu(g, _):
        gu_start(g)
        return 0
    lax.fori_loop(0, GU_SLOTS, prime_gu, 0)

    def prime_dn(g, _):
        dn_copy(g).start()
        return 0
    lax.fori_loop(0, DN_SLOTS, prime_dn, 0)

    own_local(1)

    src_row = lax.broadcasted_iota(jnp.int32, (hd, kvh * kvh * hd), 0)
    dst_col = lax.broadcasted_iota(jnp.int32, (hd, kvh * kvh * hd), 1)
    spread[...] = jnp.where(dst_col == src_row * kvh + lax.div(dst_col, kvh * hd) * (kvh * hd + 1), 1.0, 0.0).astype(BF16)
    for c in small:
        c.wait()
    for i in range(2):
        gain = gain_v[i].astype(F32)
        for l in range(L):
            gains[i, l] = gain[l:l + 1, :]

    def token_pos(t, dev):
        half = tok // 2
        return jnp.where(t < half, dev * half + t, (2 * n - 1 - dev) * half + t - half)

    def reset(st):
        m_s[st] = jnp.full((grows, hd), -jnp.inf, F32)
        l_s[st] = jnp.zeros((grows, hd), F32)
        o_s[st] = jnp.zeros((grows, hd), F32)

    def fold(st, s, pv_dot):
        width = s.shape[1]
        m_prev = m_s[st]
        m_new = jnp.maximum(m_prev, jnp.max(s, axis=1, keepdims=True))
        alpha = jnp.exp2((m_prev - m_new) * scale)
        p = jnp.exp2((s - jnp.concatenate([m_new] * (width // hd), axis=1)) * scale)
        lsum = p[:, :hd]
        for b in range(1, width // hd):
            lsum = lsum + p[:, b * hd:(b + 1) * hd]
        m_s[st] = m_new
        l_s[st] = alpha * l_s[st] + lsum
        o_s[st] = alpha * o_s[st] + pv_dot(p.astype(BF16))

    def attend_prefix(l, st, q_at, ch):
        subs = [pl.ds(pl.multiple_of(ch * COMM_CHUNK + sub * KEY_CHUNK, KEY_CHUNK), KEY_CHUNK)
                for sub in range(COMM_CHUNK // KEY_CHUNK)]
        scores = [mm(q_at(), kv[lax.rem(l, 2), 0, :, pos]) for pos in subs]
        for s, pos in zip(scores, subs):
            fold(st, s, lambda p: mm_t(p, kv[lax.rem(l, 2), 1, :, pos]))

    def attend_new(l, st, q_at, dev):
        s = mm_t(q_at(), nkv[l, 0])
        width = n * tok
        tq = lax.broadcasted_iota(jnp.int32, (grows, width), 0) & (tok - 1)
        col = lax.broadcasted_iota(jnp.int32, (grows, width), 1)
        tk = col & (tok - 1)
        dk = col >> (tok.bit_length() - 1)
        allowed = token_pos(tk, dk) <= token_pos(tq, dev)
        s = jnp.where(allowed, s, -jnp.inf)
        fold(st, s, lambda p: mm(p, nkv[l, 1]))

    def finish(st, dst):
        o = (o_s[st] / jnp.sum(l_s[st], axis=1, keepdims=True)).astype(BF16)
        for h in range(grp):
            dst[:, h * hd:(h + 1) * hd] = o[h * tok:(h + 1) * tok, :]

    own_q = pl.ds(pl.multiple_of(kvj * grows, grows), grows)
    mate_q = pl.ds(pl.multiple_of((1 - kvj) * grows, grows), grows)
    own_tok = pl.ds(pl.multiple_of(core * tok, tok), tok)
    sib_tok = pl.ds(pl.multiple_of((1 - core) * tok, tok), tok)
    my_new = pl.ds(pl.multiple_of(me * tok, tok), tok)

    def layer(l, _):
        @pl.when(l > 0)
        def _():
            forward(l, 0)
        h = rms(x_s[...], gains[0, l])
        pltpu.make_async_copy(wo.at[l], wq_v, wq_sem).wait()
        cos_t = jnp.concatenate([trig[0], trig[0]], axis=1)
        sin_t = jnp.concatenate([-trig[1], trig[1]], axis=1)

        def rope(z):
            return (z * cos_t + pltpu.roll(z, hd // 2, 1) * sin_t).astype(BF16)

        def project_q(g):
            for pair in range(grp // 2):
                y = mm(h, wq_v[:, pl.ds(pl.multiple_of(g * gcols + 2 * pair * hd, hd), 2 * hd)])
                for s in range(2):
                    row = pl.multiple_of(g * grows + (2 * pair + s) * tok, tok)
                    qs[pl.ds(row, tok), :] = rope(y[:, s * hd:(s + 1) * hd])

        project_q(1 - kvj)
        q_copy = rcopy(qs.at[mate_q, :], qr, q_sem.at[0], q_sem.at[1], mate)
        q_copy.start()
        project_q(kvj)
        hs = jnp.concatenate([h[:, b * hd:(b + 1) * hd] for b in range(D // hd)], axis=0)
        hs = mm(hs, spread[...]).astype(BF16)
        for b in range(D // hd):
            for j in range(kvh):
                wide[j * tok:(j + 1) * tok, b * kvh * hd:(b + 1) * kvh * hd] = hs[b * tok:(b + 1) * tok, j * kvh * hd:(j + 1) * kvh * hd]
        for i, src in enumerate((wk, wv)):
            pltpu.make_async_copy(src.at[l], wkv_v.at[:, pl.ds(i * hd, hd)], wkv_sem.at[i]).wait()
        y = mm(wide[...], wkv_v[...])
        for j in range(kvh):
            kvs[j, 0] = rope(y[j * tok:(j + 1) * tok, :hd])
            kvs[j, 1] = y[j * tok:(j + 1) * tok, hd:].astype(BF16)

        @pl.when(l + 1 < L)
        def _():
            wq_start(l + 1)

        for i in range(2):
            nkv[l, i, my_new, :] = kvs[kvj, i]

        def nk_copy(off):
            dst = lax.rem(me + off, n)
            return rcopy(kvs.at[lax.div(dst, per)], nkv.at[l, :, my_new, :], nk_s.at[off], nk_r.at[l, me], dst)


        @pl.when(l == 0)
        def _():
            forward(l, 0)
        full = kv.at[lax.rem(l, 2), :, my_rows, :]
        pltpu.make_async_copy(full, full, lsem.at[l]).wait()

        reset(0)
        reset(1)

        def own_chunk(ch, _):
            attend_prefix(l, 0, lambda: qs[own_q, :], ch)
            return 0

        def first_half(ch, _):
            chunk_ready(l, ch)

            @pl.when(ch == nch // 2 - 1)
            def _():
                for off in range(1, n):
                    nk_copy(off).start()

                @pl.when((l > 0) & (l + 1 < L))
                def _():
                    pl.semaphore_wait(credit.at[0], 1)
                    pl.semaphore_wait(credit.at[1], 1)

                @pl.when(l + 1 < L)
                def _():
                    own_send(l + 1)
            return own_chunk(ch, 0)
        lax.fori_loop(0, nch // 2, first_half, 0)
        q_copy.wait_recv()

        def mate_chunk(ch, _):
            @pl.when(ch >= nch // 2)
            def _():
                chunk_ready(l, ch)
            attend_prefix(l, 1, lambda: qr[...], ch)
            return 0
        lax.fori_loop(0, nch, mate_chunk, 0)
        for off in range(1, n):
            src = lax.rem(me + off, n)
            blk = nkv.at[l, :, pl.ds(pl.multiple_of(src * tok, tok), tok), :]
            rcopy(blk, blk, nk_s.at[off], nk_r.at[l, src], src).wait_recv()
        attend_new(l, 1, lambda: qr[...], mate)
        finish(1, att_snd)
        o_copy = rcopy(att_snd, att_rcv, o_sem.at[0], o_sem.at[1], mate)
        o_copy.start()
        lax.fori_loop(nch // 2, nch, own_chunk, 0)
        attend_new(l, 0, lambda: qs[own_q, :], me)
        finish(0, att_own)
        kv_free(l)

        pltpu.make_async_copy(wo.at[l], wo_v, wo_sem).wait()
        y = mm(att_own[...], wo_v[pl.ds(pl.multiple_of(kvj * gcols, gcols), gcols), :])
        o_copy.wait_recv()
        y = y + mm(att_rcv[...], wo_v[pl.ds(pl.multiple_of((1 - kvj) * gcols, gcols), gcols), :])
        x1 = (x_s[...].astype(F32) + y).astype(BF16)
        x_s[...] = x1
        h2[own_tok, :] = rms(x1, gains[1, l])
        h_copy = rcopy(h2.at[own_tok, :], h2.at[own_tok, :], h_sem.at[0], h_sem.at[1], sib)
        h_copy.start()

        q_copy.wait_send()
        o_copy.wait_send()
        for off in range(1, n):
            nk_copy(off).wait_send()
        half = tok // 2
        for i, out in enumerate((k_out, v_out)):
            pieces = [nkv[l, i, d * tok:d * tok + half, :] for d in range(n)]
            pieces += [nkv[l, i, d * tok + half:(d + 1) * tok, :] for d in reversed(range(n))]
            tr[...] = jnp.concatenate(pieces, axis=0).astype(F32).T
            newc[l, i] = tr[my_rows, :].astype(BF16)
            pltpu.make_async_copy(newc.at[l, i], out.at[l], new_sem.at[i]).start()
        h_copy.wait_recv()

        def gate_up(i):
            return mm(h2[...], gu[lax.rem(l * ngu + i, GU_SLOTS)])

        def activate(i, y):
            gate = y[:, :GU_CHUNK]
            act[:, pl.ds(gu_off(i), GU_CHUNK)] = (gate * jax.nn.sigmoid(gate) * y[:, GU_CHUNK:]).astype(BF16)

        def refill(i):
            @pl.when(l * ngu + i + GU_SLOTS < L * ngu)
            def _():
                gu_start(l * ngu + i + GU_SLOTS)

        gu_wait(l * ngu)
        activate(0, gate_up(0))
        refill(0)

        def gu_pair(k, _):
            gu_wait(l * ngu + 2 * k + 1)
            gu_wait(l * ngu + 2 * k + 2)
            ya = gate_up(2 * k + 1)
            yb = gate_up(2 * k + 2)
            activate(2 * k + 1, ya)
            activate(2 * k + 2, yb)
            refill(2 * k + 1)
            refill(2 * k + 2)
            return 0
        lax.fori_loop(0, (ngu - 1) // 2, gu_pair, 0)

        @pl.when(l + 1 < L)
        def _():
            wo_start(l + 1)

        def p_copy(i):
            return rcopy(pr.at[i, sib_tok, :], part.at[i], p_send.at[i], p_recv.at[i], sib)

        def down(k, _):
            for i in (2 * k, 2 * k + 1):
                dn_copy(l * ndn + i).wait()
            for i in (2 * k, 2 * k + 1):
                slot = lax.rem(l * ndn + i, DN_SLOTS)
                pr[i] = mm(act[:, :ksplit], w2[slot, :ksplit, :]) + mm(act[:, ksplit:], w2[slot, ksplit:, :])
            for i in (2 * k, 2 * k + 1):
                p_copy(i).start()

                @pl.when(l * ndn + i + DN_SLOTS < L * ndn)
                def _():
                    dn_copy(l * ndn + i + DN_SLOTS).start()
            return 0
        lax.fori_loop(0, ndn // 2, down, 0)
        h_copy.wait_send()
        for i in range(ndn):
            cs = slice(i * DN_CHUNK, (i + 1) * DN_CHUNK)
            mine = x_s[:, cs].astype(F32) + pr[i, own_tok, :]
            p_copy(i).wait_recv()
            x_s[:, cs] = (mine + part[i]).astype(BF16)
            p_copy(i).wait_send()
        return 0

    lax.fori_loop(0, L, layer, 0)
    out_copy = pltpu.make_async_copy(x_s, x_out, in_sem.at[0])
    out_copy.start()
    for i, out in enumerate((k_out, v_out)):
        pltpu.make_async_copy(newc.at[:, i], out, new_sem.at[i]).wait()

    def drain(l, _):
        full = kv.at[lax.rem(l, 2), :, my_rows, :]
        rcopy(full, full, ss_sib.at[l], rs_sib.at[l, 0], sib).wait_send()
        rcopy(full, full, ss_nbr.at[l], rs_nbr.at[l, 0], nbr).wait_send()
        return 0
    lax.fori_loop(0, L, drain, 0)
    out_copy.wait()


def solution(mesh):
    n = mesh.shape['cp']

    def device_fn(hidden, prefix_k, prefix_v, gain_attn, gain_mlp, w_query, w_key, w_value, w_out, w_gate, w_up, w_down):
        L, D, kvh, hd = w_key.shape
        heads = w_query.shape[2]
        tok = hidden.shape[0]
        plen = prefix_k.shape[1]
        cols = prefix_k.shape[2]
        ff = w_gate.shape[2]
        grp = heads // kvh
        half = tok // 2
        me = lax.axis_index('cp')
        pieces = jnp.stack([me, 2 * n - 1 - me])
        pos = (plen + pieces[:, None] * half + jnp.arange(half)).reshape(-1)
        inv_freq = ROPE_THETA ** (-jnp.arange(0, hd, 2, dtype=F32) / hd)
        ang = pos.astype(F32)[:, None] * inv_freq[None, :]
        cos_t = jnp.cos(ang)
        sin_t = jnp.sin(ang)
        pk = prefix_k.transpose(0, 2, 1)
        pv = prefix_v.transpose(0, 2, 1)
        wq = w_query.transpose(0, 2, 1, 3)
        wk = w_key.reshape(L, D * kvh, hd)
        wv = w_value.reshape(L, D * kvh, hd)
        wo = w_out.reshape(L, heads * hd, D)
        cfg = (n, L, D, heads, kvh, hd, tok, cols, plen)
        nch = plen // COMM_CHUNK
        rows = grp * tok
        dma = pltpu.SemaphoreType.DMA
        hbm = pl.BlockSpec(memory_space=pl.ANY)
        hid, nk, nv = pl.pallas_call(
            functools.partial(kernel, cfg),
            out_shape=(jax.ShapeDtypeStruct((tok, D), BF16),
                       jax.ShapeDtypeStruct((L, cols, n * tok), BF16),
                       jax.ShapeDtypeStruct((L, cols, n * tok), BF16)),
            in_specs=[hbm] * 14,
            out_specs=(hbm, hbm, hbm),
            scratch_shapes=[
                pltpu.VMEM((2, 2, hd, plen), BF16),
                pltpu.VMEM((GU_SLOTS, D, 2 * GU_CHUNK), BF16),
                pltpu.VMEM((DN_SLOTS, ff // 2, DN_CHUNK), BF16),
                pltpu.VMEM((D, heads * hd), BF16),
                pltpu.VMEM((D * kvh, 2 * hd), BF16),
                pltpu.VMEM((heads * hd, D), BF16),
                pltpu.VMEM((L, 2, n * tok, hd), BF16),
                pltpu.VMEM((kvh, 2, tok, hd), BF16),
                pltpu.VMEM((heads * tok, hd), BF16),
                pltpu.VMEM((rows, hd), BF16),
                pltpu.VMEM((2 * tok, D), BF16),
                pltpu.VMEM((2 * tok, ff // 2), BF16),
                pltpu.VMEM((D // DN_CHUNK, 2 * tok, DN_CHUNK), F32),
                pltpu.VMEM((D // DN_CHUNK, tok, DN_CHUNK), F32),
                pltpu.VMEM((tok, D), BF16),
                pltpu.VMEM((tok, grp * hd), BF16),
                pltpu.VMEM((tok, grp * hd), BF16),
                pltpu.VMEM((tok, grp * hd), BF16),
                pltpu.VMEM((2, rows, hd), F32),
                pltpu.VMEM((2, rows, hd), F32),
                pltpu.VMEM((2, rows, hd), F32),
                pltpu.VMEM((hd, n * tok), F32),
                pltpu.VMEM((2, L, 1, D), F32),
                pltpu.VMEM((2, L, D), BF16),
                pltpu.VMEM((2, tok, hd // 2), F32),
                pltpu.VMEM((hd, kvh * kvh * hd), BF16),
                pltpu.VMEM((kvh * tok, D * kvh), BF16),
                pltpu.VMEM((L, 2, cols, n * tok), BF16),
                dma((L,)), dma((L,)), dma((L,)), dma((L,)),
                dma((L, nch)), dma((L, nch)), dma((L, nch)),
                dma((n,)), dma((L, n)),
                dma((2,)), dma((2,)), dma((2,)), dma((D // DN_CHUNK,)), dma((D // DN_CHUNK,)),
                dma, dma((2,)), dma, dma((GU_SLOTS, 2)), dma((DN_SLOTS,)), dma((5,)), dma((2,)), pltpu.SemaphoreType.REGULAR((2,)),
            ],
            compiler_params=pltpu.CompilerParams(collective_id=0, has_side_effects=True, vmem_limit_bytes=67043328),
            name='prefill',
        )(hidden, pk, pv, gain_attn, gain_mlp, wq, wk, wv, wo, w_gate, w_up, w_down, cos_t, sin_t)
        cache_k = jnp.concatenate([pk, nk], axis=2).transpose(0, 2, 1)
        cache_v = jnp.concatenate([pv, nv], axis=2).transpose(0, 2, 1)
        return hid, cache_k, cache_v

    in_specs = (P(('req', 'cp'), None), P(None, 'req', 'cp'), P(None, 'req', 'cp')) + (P(),) * 9
    out_specs = (P(('req', 'cp'), None), P(None, 'req', 'cp'), P(None, 'req', 'cp'))
    return jax.shard_map(device_fn, mesh=mesh, in_specs=in_specs, out_specs=out_specs, check_vma=False)
```

time: 172 us -> 139 us (0.81)
  Pallas kernels: 146 us -> 132 us
  local copies, waits for them, and re-layouts: 14 us -> 0.77 us
  other arithmetic: 10.9 us -> 4.88 us
    pallas_call x1, Pallas kernels: 146 us -> 132 us  [device_fn(): pl.pallas_call(functools.partial(kernel, cfg), out_shape=(jax.ShapeDtypeS...]
    reshape x2 -> x0, local copies, waits for them, and re-layouts: 10.6 us -> none  [the longest x1 6.03 us: device_fn(): w_key.reshape(L, D, kvh * hd)]
    concatenate x2 -> x0, other arithmetic: 5.75 us -> none  [the longest x1 5.04 us: device_fn(): jnp.concatenate([w_key.reshape(L, D, kvh * hd), w_value.reshape(L, D, kvh...]
    broadcast_in_dim x2 -> x0, local copies, waits for them, and re-layouts: 2.66 us -> none  [the longest x1 1.33 us: device_fn(): g1 = gain_attn[:, None, :]]
where the time goes in v2:
time: 139 us
  Pallas kernels  132 us (95%)
  other arithmetic  4.88 us (4%)
    pallas_call x1, Pallas kernels, device_fn(): pl.pallas_call(functools.partial(kernel, cfg), out_shape=(jax.ShapeDtypeS...  132 us
    transpose x1, other arithmetic, device_fn(): cache_k = jnp.concatenate([pk, nk], axis=2).transpose(0, 2, 1)  3.89 us

profile of v2, /device:TPU:113, one launch (start us, length us, event | category | flops | bytes accessed | tf_op | source)
XLA Modules:
  0.0 138.6 jit_solution(6100032432719144096)
XLA Ops:
  0.6 0.1 fusion
  0.7 0.1 add_convert_fusion
  0.8 0.1 convert_element_type.11
  0.9 0.8 multiply_sine_fusion
  1.7 132.3 %prefill.1 = (bf16[64,1536]{1,0:T(8,128)(2,1)}, bf16[4,32,512]{2,1,0:T(8,128)(2,1)}, bf16[4,32,512]{2,1,0:T(8,128)(2,1)}) custom-call(bf16[64,1536]{1,0:T(8,128)(2,1)} %x_in.1, bf16[4,32,8192]{2,1,0:T(8,128)(2,1)} %bitcast.14, bf16[4,32,8192]{2,1,0:T(8,128)(2,1)} %bitcast.16, bf16[4,1536]{1,0:T(4,128)(2,1)} %g1.1, bf16[4,1536]{1,0:T(4,128)(2,1)} %g2.1, ...), custom_call_target="tpu_custom_call" | custom-call | tf_op jit(solution)/shard_map/prefill/pallas_call | solution.py:468
  134.0 0.0 copy-start
  134.0 3.9 %maximum_bitcast_fusion = (bf16[4,8704,32]{1,2,0:T(8,128)(2,1)}, bf16[4,8704,32]{1,2,0:T(8,128)(2,1)}) fusion(bf16[4,32,512]{2,1,0:T(8,128)(2,1)} %get-tuple-element.7, bf16[4,32,8192]{2,1,0:T(8,128)(2,1)} %bitcast.15, bf16[4,32,512]{2,1,0:T(8,128)(2,1)} %get-tuple-element.8, bf16[4,32,8192]{2,1,0:T(8,128)(2,1)} %bitcast.17), kind=kLoop, calls=%fused_computation | loop fusion | flops 8912896 | bytes 8912896 | tf_op jit(solution)/shard_map/transpose | solution.py:513
  137.9 0.0 copy-done
  137.9 0.7 copy.16
  (1 shorter events, 0.0 us)
Async XLA Ops:
  134.0 3.9 %copy-start = (bf16[64,1536]{1,0:T(8,128)(2,1)S(1)}, bf16[64,1536]{1,0:T(8,128)(2,1)}, u32[]{:S(2)}) copy-start(bf16[64,1536]{1,0:T(8,128)(2,1)} %get-tuple-element.16) | copy-start | bytes 589828

commit v3 on v2

--- a/solution.py
+++ b/solution.py
@@ -14,10 +14,12 @@
 F32 = jnp.float32
 BF16 = jnp.bfloat16
 
-COMM_CHUNK = 2048
-KEY_CHUNK = 1024
+COMM_CHUNK = 1024
+KEY_CHUNK = 512
+LOOKAHEAD = 2
 GU_CHUNK = 512
-GU_SLOTS = 6
+GU_UNROLL = 3
+GU_SLOTS = 7
 DN_CHUNK = 256
 DN_SLOTS = 6
 
@@ -39,8 +41,8 @@
 def kernel(cfg, x_in, pk, pv, g1, g2, wq, wk, wv, wo, wg, wu, wd, cos_ref, sin_ref,
            x_out, k_out, v_out,
            kv, gu, w2, wq_v, wkv_v, wo_v, nkv, kvs, qs, qr, h2, act, pr, part, x_s, att_own, att_snd, att_rcv,
-           m_s, l_s, o_s, tr, gains, gain_v, trig, spread, wide, newc,
-           lsem, ss_sib, ss_nbr, ss_fwd, rs_sib, rs_nbr, rs_fwd, nk_s, nk_r, q_sem, o_sem, h_sem, p_send, p_recv,
+           m_s, l_s, o_s, tr, gains, gain_v, trig, spread, newc,
+           lsem, ss_sib, ss_nbr, ss_fwd, rs_sib, rs_nbr, rs_fwd, nk_s, nk_f, nk_r, q_sem, o_sem, h_sem, p_send, p_recv,
            wq_sem, wkv_sem, wo_sem, gu_sem, w2_sem, in_sem, new_sem, credit):
     n, L, D, heads, kvh, hd, tok, cols, plen = cfg
     grp = heads // kvh
@@ -124,23 +126,24 @@
         def body(ch, _):
             for i, src in enumerate((pk, pv)):
                 rcopy(src.at[l, :, cpos(ch)], kv.at[b, i, my_rows, cpos(ch)], ss_nbr.at[l], rs_nbr.at[l, ch], nbr).start()
-                rcopy(src.at[l, :, cpos(ch)], kv.at[b, i, my_rows, cpos(ch)], ss_sib.at[l], rs_sib.at[l, ch], sib).start()
             return 0
         lax.fori_loop(0, nch, body, 0)
+        for i, src in enumerate((pk, pv)):
+            rcopy(src.at[l], kv.at[b, i, my_rows, :], ss_sib.at[l], rs_sib.at[l], sib).start()
 
     def forward(l, ch):
         blk = kv.at[lax.rem(l, 2), :, nbr_rows, cpos(ch)]
         rcopy(blk, blk, ss_nbr.at[l], rs_nbr.at[l, ch], nbr).wait_recv()
         rcopy(blk, blk, ss_fwd.at[l], rs_fwd.at[l, ch], sib).start()
 
-    def chunk_ready(l, ch):
-        @pl.when(ch + 1 < nch)
-        def _():
-            forward(l, ch + 1)
-        blk = kv.at[lax.rem(l, 2), :, sib_rows, cpos(ch)]
-        rcopy(blk, blk, ss_sib.at[l], rs_sib.at[l, ch], sib).wait_recv()
+    def chunk_wait(l, ch):
         blk = kv.at[lax.rem(l, 2), :, sibnbr_rows, cpos(ch)]
         rcopy(blk, blk, ss_fwd.at[l], rs_fwd.at[l, ch], sib).wait_recv()
+
+    def forward_next(l, ch):
+        @pl.when(l + 1 < L)
+        def _():
+            forward(l + 1, ch)
 
     def kv_free(l):
         full = kv.at[lax.rem(l, 2), :, nbr_rows, :]
@@ -197,52 +200,60 @@
         l_s[st] = jnp.zeros((grows, hd), F32)
         o_s[st] = jnp.zeros((grows, hd), F32)
 
-    def fold(st, s, pv_dot):
+    def fold(st, at, s, pv_dot):
         width = s.shape[1]
-        m_prev = m_s[st]
+        m_prev = m_s[st, at, :]
         m_new = jnp.maximum(m_prev, jnp.max(s, axis=1, keepdims=True))
         alpha = jnp.exp2((m_prev - m_new) * scale)
         p = jnp.exp2((s - jnp.concatenate([m_new] * (width // hd), axis=1)) * scale)
         lsum = p[:, :hd]
         for b in range(1, width // hd):
             lsum = lsum + p[:, b * hd:(b + 1) * hd]
-        m_s[st] = m_new
-        l_s[st] = alpha * l_s[st] + lsum
-        o_s[st] = alpha * o_s[st] + pv_dot(p.astype(BF16))
-
-    def attend_prefix(l, st, q_at, ch):
-        subs = [pl.ds(pl.multiple_of(ch * COMM_CHUNK + sub * KEY_CHUNK, KEY_CHUNK), KEY_CHUNK)
-                for sub in range(COMM_CHUNK // KEY_CHUNK)]
-        scores = [mm(q_at(), kv[lax.rem(l, 2), 0, :, pos]) for pos in subs]
-        for s, pos in zip(scores, subs):
-            fold(st, s, lambda p: mm_t(p, kv[lax.rem(l, 2), 1, :, pos]))
-
-    def attend_new(l, st, q_at, dev):
-        s = mm_t(q_at(), nkv[l, 0])
-        width = n * tok
-        tq = lax.broadcasted_iota(jnp.int32, (grows, width), 0) & (tok - 1)
-        col = lax.broadcasted_iota(jnp.int32, (grows, width), 1)
-        tk = col & (tok - 1)
-        dk = col >> (tok.bit_length() - 1)
-        allowed = token_pos(tk, dk) <= token_pos(tq, dev)
-        s = jnp.where(allowed, s, -jnp.inf)
-        fold(st, s, lambda p: mm(p, nkv[l, 1]))
-
-    def finish(st, dst):
-        o = (o_s[st] / jnp.sum(l_s[st], axis=1, keepdims=True)).astype(BF16)
-        for h in range(grp):
-            dst[:, h * hd:(h + 1) * hd] = o[h * tok:(h + 1) * tok, :]
+        m_s[st, at, :] = m_new
+        l_s[st, at, :] = alpha * l_s[st, at, :] + lsum
+        o_s[st, at, :] = alpha * o_s[st, at, :] + pv_dot(p.astype(BF16))
+
+    def sweep(l, jobs):
+        b = lax.rem(l, 2)
+
+        def keys(first):
+            return pl.ds(first if isinstance(first, int) else pl.multiple_of(first, KEY_CHUNK), KEY_CHUNK)
+
+        def score(job):
+            _, at, q, first, dev = job
+            if first is not None:
+                return mm(q(), kv[b, 0, :, keys(first)])
+            s = mm_t(q(), nkv[lax.rem(l, 2), 0])
+            width = n * tok
+            shape = (at.stop - at.start, width)
+            tq = lax.broadcasted_iota(jnp.int32, shape, 0) & (tok - 1)
+            col = lax.broadcasted_iota(jnp.int32, shape, 1)
+            tk = col & (tok - 1)
+            dk = col >> (tok.bit_length() - 1)
+            return jnp.where(token_pos(tk, dk) <= token_pos(tq, dev), s, -jnp.inf)
+
+        def mix(job):
+            if job[3] is not None:
+                return lambda p: mm_t(p, kv[b, 1, :, keys(job[3])])
+            return lambda p: mm(p, nkv[lax.rem(l, 2), 1])
+
+        ahead = [score(job) for job in jobs[:LOOKAHEAD]]
+        for i, job in enumerate(jobs):
+            fold(job[0], job[1], ahead.pop(0), mix(job))
+            if i + LOOKAHEAD < len(jobs):
+                ahead.append(score(jobs[i + LOOKAHEAD]))
+
+    def finish(st, dst, first, last):
+        o = (o_s[st, first * tok:last * tok, :] / jnp.sum(l_s[st, first * tok:last * tok, :], axis=1, keepdims=True)).astype(BF16)
+        for h in range(first, last):
+            dst[:, h * hd:(h + 1) * hd] = o[(h - first) * tok:(h - first + 1) * tok, :]
 
     own_q = pl.ds(pl.multiple_of(kvj * grows, grows), grows)
-    mate_q = pl.ds(pl.multiple_of((1 - kvj) * grows, grows), grows)
     own_tok = pl.ds(pl.multiple_of(core * tok, tok), tok)
     sib_tok = pl.ds(pl.multiple_of((1 - core) * tok, tok), tok)
     my_new = pl.ds(pl.multiple_of(me * tok, tok), tok)
 
     def layer(l, _):
-        @pl.when(l > 0)
-        def _():
-            forward(l, 0)
         h = rms(x_s[...], gains[0, l])
         pltpu.make_async_copy(wo.at[l], wq_v, wq_sem).wait()
         cos_t = jnp.concatenate([trig[0], trig[0]], axis=1)
@@ -251,25 +262,29 @@
         def rope(z):
             return (z * cos_t + pltpu.roll(z, hd // 2, 1) * sin_t).astype(BF16)
 
-        def project_q(g):
+        def q_copy(pair):
+            at = pl.ds(pl.multiple_of((1 - kvj) * grows + 2 * pair * tok, 2 * tok), 2 * tok)
+            return rcopy(qs.at[at, :], qr.at[pl.ds(2 * pair * tok, 2 * tok), :], q_sem.at[0, pair], q_sem.at[1, pair], mate)
+
+        def project_q(g, send):
             for pair in range(grp // 2):
                 y = mm(h, wq_v[:, pl.ds(pl.multiple_of(g * gcols + 2 * pair * hd, hd), 2 * hd)])
                 for s in range(2):
                     row = pl.multiple_of(g * grows + (2 * pair + s) * tok, tok)
                     qs[pl.ds(row, tok), :] = rope(y[:, s * hd:(s + 1) * hd])
-
-        project_q(1 - kvj)
-        q_copy = rcopy(qs.at[mate_q, :], qr, q_sem.at[0], q_sem.at[1], mate)
-        q_copy.start()
-        project_q(kvj)
+                if send:
+                    q_copy(pair).start()
+
+        project_q(1 - kvj, True)
+        project_q(kvj, False)
         hs = jnp.concatenate([h[:, b * hd:(b + 1) * hd] for b in range(D // hd)], axis=0)
         hs = mm(hs, spread[...]).astype(BF16)
         for b in range(D // hd):
             for j in range(kvh):
-                wide[j * tok:(j + 1) * tok, b * kvh * hd:(b + 1) * kvh * hd] = hs[b * tok:(b + 1) * tok, j * kvh * hd:(j + 1) * kvh * hd]
+                act[j * tok:(j + 1) * tok, b * kvh * hd:(b + 1) * kvh * hd] = hs[b * tok:(b + 1) * tok, j * kvh * hd:(j + 1) * kvh * hd]
         for i, src in enumerate((wk, wv)):
             pltpu.make_async_copy(src.at[l], wkv_v.at[:, pl.ds(i * hd, hd)], wkv_sem.at[i]).wait()
-        y = mm(wide[...], wkv_v[...])
+        y = mm(act[:kvh * tok, :kvh * D], wkv_v[...])
         for j in range(kvh):
             kvs[j, 0] = rope(y[j * tok:(j + 1) * tok, :hd])
             kvs[j, 1] = y[j * tok:(j + 1) * tok, hd:].astype(BF16)
@@ -279,69 +294,129 @@
             wq_start(l + 1)
 
         for i in range(2):
-            nkv[l, i, my_new, :] = kvs[kvj, i]
-
-        def nk_copy(off):
-            dst = lax.rem(me + off, n)
-            return rcopy(kvs.at[lax.div(dst, per)], nkv.at[l, :, my_new, :], nk_s.at[off], nk_r.at[l, me], dst)
-
-
-        @pl.when(l == 0)
-        def _():
-            forward(l, 0)
+            nkv[lax.rem(l, 2), i, my_new, :] = kvs[kvj, i]
+
+        def new_rows(src):
+            return nkv.at[lax.rem(l, 2), :, pl.ds(pl.multiple_of(src * tok, tok), tok), :]
+
+        def nk_copy(k):
+            dst = lax.rem(me + 2 * k, n) if k else sib
+            return rcopy(kvs.at[lax.div(dst, per)], nkv.at[lax.rem(l, 2), :, my_new, :], nk_s.at[k], nk_r.at[l, me], dst)
+
+        def nk_relay(k):
+            src = lax.rem(me + 2 * k, n)
+            return rcopy(new_rows(src), new_rows(src), nk_f.at[k], nk_r.at[l, src], sib)
+
+        def relay_new():
+            for k in range(1, n // 2):
+                src = lax.rem(me + 2 * k, n)
+                rcopy(new_rows(src), new_rows(src), nk_s.at[k], nk_r.at[l, src], src).wait_recv()
+                nk_relay(k).start()
+
+        def new_ready():
+            for k in range(n // 2):
+                src = lax.rem(sib + 2 * k, n)
+                rcopy(new_rows(src), new_rows(src), nk_s.at[k], nk_r.at[l, src], sib).wait_recv()
+
+        for k in range(n // 2):
+            nk_copy(k).start()
+
+        @pl.when((l > 0) & (l + 1 < L))
+        def _():
+            pl.semaphore_wait(credit.at[0], 1)
+            pl.semaphore_wait(credit.at[1], 1)
+
+        @pl.when(l + 1 < L)
+        def _():
+            own_send(l + 1)
+
         full = kv.at[lax.rem(l, 2), :, my_rows, :]
         pltpu.make_async_copy(full, full, lsem.at[l]).wait()
-
+        full = kv.at[lax.rem(l, 2), :, sib_rows, :]
+        rcopy(full, full, ss_sib.at[l], rs_sib.at[l], sib).wait_recv()
         reset(0)
         reset(1)
-
-        def own_chunk(ch, _):
-            attend_prefix(l, 0, lambda: qs[own_q, :], ch)
-            return 0
-
-        def first_half(ch, _):
-            chunk_ready(l, ch)
-
-            @pl.when(ch == nch // 2 - 1)
-            def _():
-                for off in range(1, n):
-                    nk_copy(off).start()
-
-                @pl.when((l > 0) & (l + 1 < L))
-                def _():
-                    pl.semaphore_wait(credit.at[0], 1)
-                    pl.semaphore_wait(credit.at[1], 1)
-
-                @pl.when(l + 1 < L)
-                def _():
-                    own_send(l + 1)
-            return own_chunk(ch, 0)
-        lax.fori_loop(0, nch // 2, first_half, 0)
-        q_copy.wait_recv()
-
-        def mate_chunk(ch, _):
-            @pl.when(ch >= nch // 2)
-            def _():
-                chunk_ready(l, ch)
-            attend_prefix(l, 1, lambda: qr[...], ch)
-            return 0
-        lax.fori_loop(0, nch, mate_chunk, 0)
-        for off in range(1, n):
-            src = lax.rem(me + off, n)
-            blk = nkv.at[l, :, pl.ds(pl.multiple_of(src * tok, tok), tok), :]
-            rcopy(blk, blk, nk_s.at[off], nk_r.at[l, src], src).wait_recv()
-        attend_new(l, 1, lambda: qr[...], mate)
-        finish(1, att_snd)
-        o_copy = rcopy(att_snd, att_rcv, o_sem.at[0], o_sem.at[1], mate)
-        o_copy.start()
-        lax.fori_loop(nch // 2, nch, own_chunk, 0)
-        attend_new(l, 0, lambda: qs[own_q, :], me)
-        finish(0, att_own)
+        halves = (0, grp // 2, grp)
+
+        def o_copy(i):
+            at = pl.ds(halves[i] * hd, (halves[i + 1] - halves[i]) * hd)
+            return rcopy(att_snd.at[:, at], att_rcv.at[:, at], o_sem.at[0, i], o_sem.at[1, i], mate)
+
+        def own_job(first):
+            return (0, slice(0, grows), lambda: qs[own_q, :], first, me)
+
+        def mate_job(first, at=slice(0, grows)):
+            return (1, at, lambda: qr[at, :], first, mate)
+
+        def blocks(first, last):
+            return [first + k * KEY_CHUNK for k in range((last - first) // KEY_CHUNK)]
+
+        def mate_tail(firsts):
+            for i in range(2):
+                at = slice(halves[i] * tok, halves[i + 1] * tok)
+                sweep(l, [mate_job(f, at) for f in firsts] + [mate_job(None, at)])
+                finish(1, att_snd, halves[i], halves[i + 1])
+                o_copy(i).start()
+
+        @pl.when(l == 0)
+        def _():
+            for pair in range(grp // 2):
+                q_copy(pair).wait_recv()
+
+            def arrive(ch, _):
+                forward(l, ch)
+                chunk_wait(l, ch)
+                first = ch * COMM_CHUNK
+                firsts = [first + k * KEY_CHUNK for k in range(COMM_CHUNK // KEY_CHUNK)]
+                sweep(l, [own_job(f) for f in firsts] + [mate_job(f) for f in firsts])
+                return 0
+            lax.fori_loop(0, nch - 1, arrive, 0)
+            relay_new()
+            forward(l, nch - 1)
+            chunk_wait(l, nch - 1)
+            new_ready()
+            tail = blocks((nch - 1) * COMM_CHUNK, plen)
+            mate_tail(tail)
+            sweep(l, [own_job(f) for f in tail] + [own_job(None)])
+
+        @pl.when(l > 0)
+        def _():
+            forward(l, nch - 2)
+            mid = nch // 2 * COMM_CHUNK
+            for ch in range(nch // 2):
+                chunk_wait(l, ch)
+            early = (nch * 3 // 8) * COMM_CHUNK
+            sweep(l, [own_job(f) for f in blocks(0, early)])
+            for pair in range(grp // 2):
+                q_copy(pair).wait_recv()
+            sweep(l, [mate_job(f) for f in blocks(0, mid)])
+            relay_new()
+            forward(l, nch - 1)
+            for ch in range(nch // 2, nch * 3 // 4):
+                chunk_wait(l, ch)
+            late = (nch * 3 // 4) * COMM_CHUNK
+            sweep(l, [mate_job(f) for f in blocks(mid, late)])
+            new_ready()
+            for ch in range(nch * 3 // 4, nch):
+                chunk_wait(l, ch)
+            mate_tail(blocks(late, plen))
+            sweep(l, [own_job(f) for f in blocks(early, plen)] + [own_job(None)])
+        finish(0, att_own, 0, grp)
         kv_free(l)
+        forward_next(l, 0)
+        forward_next(l, 1)
 
         pltpu.make_async_copy(wo.at[l], wo_v, wo_sem).wait()
         y = mm(att_own[...], wo_v[pl.ds(pl.multiple_of(kvj * gcols, gcols), gcols), :])
-        o_copy.wait_recv()
+        half = tok // 2
+        for i, out in enumerate((k_out, v_out)):
+            pieces = [nkv[lax.rem(l, 2), i, d * tok:d * tok + half, :] for d in range(n)]
+            pieces += [nkv[lax.rem(l, 2), i, d * tok + half:(d + 1) * tok, :] for d in reversed(range(n))]
+            tr[...] = jnp.concatenate(pieces, axis=0).astype(F32).T
+            newc[l, i] = tr[my_rows, :].astype(BF16)
+            pltpu.make_async_copy(newc.at[l, i], out.at[l], new_sem.at[i]).start()
+        for i in range(2):
+            o_copy(i).wait_recv()
         y = y + mm(att_rcv[...], wo_v[pl.ds(pl.multiple_of((1 - kvj) * gcols, gcols), gcols), :])
         x1 = (x_s[...].astype(F32) + y).astype(BF16)
         x_s[...] = x1
@@ -349,17 +424,14 @@
         h_copy = rcopy(h2.at[own_tok, :], h2.at[own_tok, :], h_sem.at[0], h_sem.at[1], sib)
         h_copy.start()
 
-        q_copy.wait_send()
-        o_copy.wait_send()
-        for off in range(1, n):
-            nk_copy(off).wait_send()
-        half = tok // 2
-        for i, out in enumerate((k_out, v_out)):
-            pieces = [nkv[l, i, d * tok:d * tok + half, :] for d in range(n)]
-            pieces += [nkv[l, i, d * tok + half:(d + 1) * tok, :] for d in reversed(range(n))]
-            tr[...] = jnp.concatenate(pieces, axis=0).astype(F32).T
-            newc[l, i] = tr[my_rows, :].astype(BF16)
-            pltpu.make_async_copy(newc.at[l, i], out.at[l], new_sem.at[i]).start()
+        for pair in range(grp // 2):
+            q_copy(pair).wait_send()
+        for i in range(2):
+            o_copy(i).wait_send()
+        for k in range(n // 2):
+            nk_copy(k).wait_send()
+        for k in range(1, n // 2):
+            nk_relay(k).wait_send()
         h_copy.wait_recv()
 
         def gate_up(i):
@@ -374,25 +446,26 @@
             def _():
                 gu_start(l * ngu + i + GU_SLOTS)
 
-        gu_wait(l * ngu)
-        activate(0, gate_up(0))
-        refill(0)
-
-        def gu_pair(k, _):
-            gu_wait(l * ngu + 2 * k + 1)
-            gu_wait(l * ngu + 2 * k + 2)
-            ya = gate_up(2 * k + 1)
-            yb = gate_up(2 * k + 2)
-            activate(2 * k + 1, ya)
-            activate(2 * k + 2, yb)
-            refill(2 * k + 1)
-            refill(2 * k + 2)
-            return 0
-        lax.fori_loop(0, (ngu - 1) // 2, gu_pair, 0)
+        for first in range(0, ngu, GU_UNROLL):
+            steps = range(first, min(first + GU_UNROLL, ngu))
+            for i in steps:
+                gu_wait(l * ngu + i)
+            ys = []
+            for i in steps:
+                ys.append(gate_up(i))
+                if i + GU_SLOTS < ngu:
+                    gu_start(l * ngu + i + GU_SLOTS)
+            for i, y in zip(steps, ys):
+                activate(i, y)
+            for i in steps:
+                if i + GU_SLOTS >= ngu:
+                    refill(i)
 
         @pl.when(l + 1 < L)
         def _():
             wo_start(l + 1)
+        for ch in range(2, 5):
+            forward_next(l, ch)
 
         def p_copy(i):
             return rcopy(pr.at[i, sib_tok, :], part.at[i], p_send.at[i], p_recv.at[i], sib)
@@ -412,6 +485,8 @@
             return 0
         lax.fori_loop(0, ndn // 2, down, 0)
         h_copy.wait_send()
+        for ch in range(5, nch - 2):
+            forward_next(l, ch)
         for i in range(ndn):
             cs = slice(i * DN_CHUNK, (i + 1) * DN_CHUNK)
             mine = x_s[:, cs].astype(F32) + pr[i, own_tok, :]
@@ -428,7 +503,7 @@
 
     def drain(l, _):
         full = kv.at[lax.rem(l, 2), :, my_rows, :]
-        rcopy(full, full, ss_sib.at[l], rs_sib.at[l, 0], sib).wait_send()
+        rcopy(full, full, ss_sib.at[l], rs_sib.at[l], sib).wait_send()
         rcopy(full, full, ss_nbr.at[l], rs_nbr.at[l, 0], nbr).wait_send()
         return 0
     lax.fori_loop(0, L, drain, 0)
@@ -479,7 +554,7 @@
                 pltpu.VMEM((D, heads * hd), BF16),
                 pltpu.VMEM((D * kvh, 2 * hd), BF16),
                 pltpu.VMEM((heads * hd, D), BF16),
-                pltpu.VMEM((L, 2, n * tok, hd), BF16),
+                pltpu.VMEM((2, 2, n * tok, hd), BF16),
                 pltpu.VMEM((kvh, 2, tok, hd), BF16),
                 pltpu.VMEM((heads * tok, hd), BF16),
                 pltpu.VMEM((rows, hd), BF16),
@@ -499,12 +574,11 @@
                 pltpu.VMEM((2, L, D), BF16),
                 pltpu.VMEM((2, tok, hd // 2), F32),
                 pltpu.VMEM((hd, kvh * kvh * hd), BF16),
-                pltpu.VMEM((kvh * tok, D * kvh), BF16),
                 pltpu.VMEM((L, 2, cols, n * tok), BF16),
                 dma((L,)), dma((L,)), dma((L,)), dma((L,)),
-                dma((L, nch)), dma((L, nch)), dma((L, nch)),
-                dma((n,)), dma((L, n)),
-                dma((2,)), dma((2,)), dma((2,)), dma((D // DN_CHUNK,)), dma((D // DN_CHUNK,)),
+                dma((L,)), dma((L, nch)), dma((L, nch)),
+                dma((n // 2,)), dma((n // 2,)), dma((L, n)),
+                dma((2, grp // 2)), dma((2, 2)), dma((2,)), dma((D // DN_CHUNK,)), dma((D // DN_CHUNK,)),
                 dma, dma((2,)), dma, dma((GU_SLOTS, 2)), dma((DN_SLOTS,)), dma((5,)), dma((2,)), pltpu.SemaphoreType.REGULAR((2,)),
             ],
             compiler_params=pltpu.CompilerParams(collective_id=0, has_side_effects=True, vmem_limit_bytes=67043328),

time: 139 us -> 133 us (0.957)
  Pallas kernels: 132 us -> 126 us
    pallas_call x1, Pallas kernels: 132 us -> 126 us  [device_fn(): pl.pallas_call(functools.partial(kernel, cfg), out_shape=(jax.ShapeDtypeS...]
where the time goes in v3:
time: 133 us; the launch traced here: 132 us
  Pallas kernels  126 us (95%)
  other arithmetic  4.88 us (4%)
    pallas_call x1, Pallas kernels, device_fn(): pl.pallas_call(functools.partial(kernel, cfg), out_shape=(jax.ShapeDtypeS...  126 us
    transpose x1, other arithmetic, device_fn(): cache_k = jnp.concatenate([pk, nk], axis=2).transpose(0, 2, 1)  3.89 us

profile of v3, /device:TPU:113, one launch (start us, length us, event | category | flops | bytes accessed | tf_op | source)
XLA Modules:
  0.0 132.4 jit_solution(11583418861053957395)
XLA Ops:
  0.6 0.1 fusion
  0.7 0.1 add_convert_fusion
  0.8 0.1 convert_element_type.11
  0.9 0.8 multiply_sine_fusion
  1.7 126.2 %prefill.1 = (bf16[64,1536]{1,0:T(8,128)(2,1)}, bf16[4,32,512]{2,1,0:T(8,128)(2,1)}, bf16[4,32,512]{2,1,0:T(8,128)(2,1)}) custom-call(bf16[64,1536]{1,0:T(8,128)(2,1)} %x_in.1, bf16[4,32,8192]{2,1,0:T(8,128)(2,1)} %bitcast.14, bf16[4,32,8192]{2,1,0:T(8,128)(2,1)} %bitcast.16, bf16[4,1536]{1,0:T(4,128)(2,1)} %g1.1, bf16[4,1536]{1,0:T(4,128)(2,1)} %g2.1, ...), custom_call_target="tpu_custom_call" | custom-call | tf_op jit(solution)/shard_map/prefill/pallas_call | solution.py:543
  127.9 0.0 copy-start
  127.9 3.9 %maximum_bitcast_fusion = (bf16[4,8704,32]{1,2,0:T(8,128)(2,1)}, bf16[4,8704,32]{1,2,0:T(8,128)(2,1)}) fusion(bf16[4,32,512]{2,1,0:T(8,128)(2,1)} %get-tuple-element.7, bf16[4,32,8192]{2,1,0:T(8,128)(2,1)} %bitcast.15, bf16[4,32,512]{2,1,0:T(8,128)(2,1)} %get-tuple-element.8, bf16[4,32,8192]{2,1,0:T(8,128)(2,1)} %bitcast.17), kind=kLoop, calls=%fused_computation | loop fusion | flops 8912896 | bytes 8912896 | tf_op jit(solution)/shard_map/transpose | solution.py:587
  131.8 0.0 copy-done
  131.8 0.7 copy.16
  (1 shorter events, 0.0 us)
Async XLA Ops:
  127.9 3.9 %copy-start = (bf16[64,1536]{1,0:T(8,128)(2,1)S(1)}, bf16[64,1536]{1,0:T(8,128)(2,1)}, u32[]{:S(2)}) copy-start(bf16[64,1536]{1,0:T(8,128)(2,1)} %get-tuple-element.16) | copy-start | bytes 589828

commit v4 on v3

--- a/solution.py
+++ b/solution.py
@@ -3,6 +3,7 @@
 
 import jax
 import jax.numpy as jnp
+import numpy as np
 from jax import lax
 from jax.experimental import pallas as pl
 from jax.experimental.pallas import tpu as pltpu
@@ -160,7 +161,9 @@
         pl.semaphore_signal(barrier, inc=1, device_id={'cp': lax.rem(me + off, n)}, device_id_type=MESH)
 
     small = [pltpu.make_async_copy(src, dst, in_sem.at[i]) for i, (src, dst) in enumerate(
-        ((x_in, x_s), (g1, gain_v.at[0]), (g2, gain_v.at[1]), (cos_ref, trig.at[0]), (sin_ref, trig.at[1])))]
+        [(x_in, x_s), (g1, gain_v.at[0]), (g2, gain_v.at[1])]
+        + [(tab.at[pl.ds(pl.multiple_of(piece * (tok // 2), tok // 2), tok // 2), :], trig.at[t, pl.ds(p * (tok // 2), tok // 2), :])
+           for t, tab in enumerate((cos_ref, sin_ref)) for p, piece in enumerate((me, 2 * n - 1 - me))])]
     for c in small:
         c.start()
     wq_start(0)
@@ -521,14 +524,10 @@
         cols = prefix_k.shape[2]
         ff = w_gate.shape[2]
         grp = heads // kvh
-        half = tok // 2
-        me = lax.axis_index('cp')
-        pieces = jnp.stack([me, 2 * n - 1 - me])
-        pos = (plen + pieces[:, None] * half + jnp.arange(half)).reshape(-1)
-        inv_freq = ROPE_THETA ** (-jnp.arange(0, hd, 2, dtype=F32) / hd)
-        ang = pos.astype(F32)[:, None] * inv_freq[None, :]
-        cos_t = jnp.cos(ang)
-        sin_t = jnp.sin(ang)
+        inv_freq = ROPE_THETA ** (-np.arange(0, hd, 2, dtype=np.float32) / np.float32(hd))
+        ang = (plen + np.arange(n * tok)).astype(np.float32)[:, None] * inv_freq.astype(np.float32)[None, :]
+        cos_t = np.cos(ang.astype(np.float64)).astype(np.float32)
+        sin_t = np.sin(ang.astype(np.float64)).astype(np.float32)
         pk = prefix_k.transpose(0, 2, 1)
         pv = prefix_v.transpose(0, 2, 1)
         wq = w_query.transpose(0, 2, 1, 3)
@@ -579,11 +578,11 @@
                 dma((L,)), dma((L, nch)), dma((L, nch)),
                 dma((n // 2,)), dma((n // 2,)), dma((L, n)),
                 dma((2, grp // 2)), dma((2, 2)), dma((2,)), dma((D // DN_CHUNK,)), dma((D // DN_CHUNK,)),
-                dma, dma((2,)), dma, dma((GU_SLOTS, 2)), dma((DN_SLOTS,)), dma((5,)), dma((2,)), pltpu.SemaphoreType.REGULAR((2,)),
+                dma, dma((2,)), dma, dma((GU_SLOTS, 2)), dma((DN_SLOTS,)), dma((7,)), dma((2,)), pltpu.SemaphoreType.REGULAR((2,)),
             ],
             compiler_params=pltpu.CompilerParams(collective_id=0, has_side_effects=True, vmem_limit_bytes=67043328),
             name='prefill',
-        )(hidden, pk, pv, gain_attn, gain_mlp, wq, wk, wv, wo, w_gate, w_up, w_down, cos_t, sin_t)
+        )(hidden, pk, pv, gain_attn, gain_mlp, wq, wk, wv, wo, w_gate, w_up, w_down, jnp.asarray(cos_t), jnp.asarray(sin_t))
         cache_k = jnp.concatenate([pk, nk], axis=2).transpose(0, 2, 1)
         cache_v = jnp.concatenate([pv, nv], axis=2).transpose(0, 2, 1)
         return hid, cache_k, cache_v

time: 133 us -> 132 us (level)
  no operation moved by 1% of the time
where the time goes in v4:
time: 132 us; the launch traced here: 131 us
  Pallas kernels  126 us (95%)
  other arithmetic  3.89 us (3%)
    pallas_call x1, Pallas kernels, device_fn(): pl.pallas_call(functools.partial(kernel, cfg), out_shape=(jax.ShapeDtypeS...  126 us
    transpose x1, other arithmetic, device_fn(): cache_k = jnp.concatenate([pk, nk], axis=2).transpose(0, 2, 1)  3.89 us

profile of v4, /device:TPU:113, one launch (start us, length us, event | category | flops | bytes accessed | tf_op | source)
XLA Modules:
  0.0 131.5 jit_solution(8321772592312449531)
XLA Ops:
  0.6 126.3 %prefill.1 = (bf16[64,1536]{1,0:T(8,128)(2,1)}, bf16[4,32,512]{2,1,0:T(8,128)(2,1)}, bf16[4,32,512]{2,1,0:T(8,128)(2,1)}) custom-call(bf16[64,1536]{1,0:T(8,128)(2,1)} %x_in.1, bf16[4,32,8192]{2,1,0:T(8,128)(2,1)} %bitcast.12, bf16[4,32,8192]{2,1,0:T(8,128)(2,1)} %bitcast.14, bf16[4,1536]{1,0:T(4,128)(2,1)} %g1.1, bf16[4,1536]{1,0:T(4,128)(2,1)} %g2.1, ...), custom_call_target="tpu_custom_call" | custom-call | tf_op jit(solution)/shard_map/prefill/pallas_call | solution.py:542
  126.9 0.0 copy-start
  126.9 3.9 %maximum_bitcast_fusion = (bf16[4,8704,32]{1,2,0:T(8,128)(2,1)}, bf16[4,8704,32]{1,2,0:T(8,128)(2,1)}) fusion(bf16[4,32,512]{2,1,0:T(8,128)(2,1)} %get-tuple-element.7, bf16[4,32,8192]{2,1,0:T(8,128)(2,1)} %bitcast.13, bf16[4,32,512]{2,1,0:T(8,128)(2,1)} %get-tuple-element.8, bf16[4,32,8192]{2,1,0:T(8,128)(2,1)} %bitcast.15), kind=kLoop, calls=%fused_computation | loop fusion | flops 8912896 | bytes 8912896 | tf_op jit(solution)/shard_map/transpose | solution.py:586
  130.8 0.0 copy-done
  130.8 0.7 copy.18
Async XLA Ops:
  126.9 3.9 %copy-start = (bf16[64,1536]{1,0:T(8,128)(2,1)S(1)}, bf16[64,1536]{1,0:T(8,128)(2,1)}, u32[]{:S(2)}) copy-start(bf16[64,1536]{1,0:T(8,128)(2,1)} %get-tuple-element.14) | copy-start | bytes 589828
